TPU v7x, 128 devices: a whole 4x4x4 slice. The times are simulated.
128 devices in a mesh: third: 4 (over z), second: 4 (over y), group: 8 (over x, core).
Axes of the slice: x: 4, y: 4, z: 4, core: 2. Of those that a mesh axis runs over, the one named last changes fastest.
Arguments:
- x_one: bfloat16 [16384, 2048], P(('third', 'second', 'group'))
- z_one: bfloat16 [16384, 8192], P(('third', 'second', 'group'))
- x_two: bfloat16 [16384, 2048], P(('third', 'second', 'group'))
- z_two: bfloat16 [16384, 8192], P(('third', 'second', 'group'))
- grad_out: bfloat16 [16384, 2048], P(('third', 'second', 'group'))
- w1_in: bfloat16 [2048, 8192], replicated
- w1_out: bfloat16 [8192, 2048], replicated
- w2_in: bfloat16 [2048, 8192], replicated
- w2_out: bfloat16 [8192, 2048], replicated
Outputs:
- output 1: float32 [8192, 2048], replicated
- output 2: float32 [2048, 8192], replicated
- output 3: float32 [8192, 2048], replicated
- output 4: float32 [2048, 8192], replicated
- output 5: bfloat16 [16384, 2048], P(('third', 'second', 'group'))
All inputs are finite; a program needn't handle non-finite values.
Results may differ from a plain program's by a relative error of at most 0.00524652.
Values are sent between devices in bfloat16 or wider.
A program may use at most 1.5 GiB of HBM per device.

v0:
```python
import math
import jax
import jax.numpy as jnp
from jax import lax
from jax.sharding import PartitionSpec as P

AXES = ('third', 'second', 'group')
INV_ROOT_TWO = math.sqrt(0.5)
INV_ROOT_TWO_PI = 1.0 / math.sqrt(2.0 * math.pi)
CONTRACT_ROWS = (((0,), (0,)), ((), ()))
CONTRACT_COLS = (((1,), (1,)), ((), ()))


def gelu_pair(z_pre):
    z_val = z_pre.astype(jnp.float32)
    cdf_val = 0.5 * (1.0 + lax.erf(z_val * INV_ROOT_TWO))
    hidden = (z_val * cdf_val).astype(jnp.bfloat16)
    slope = cdf_val + z_val * jnp.exp(-0.5 * z_val * z_val) * INV_ROOT_TWO_PI
    return hidden, slope


def block_backward(x_in, z_pre, grad_y, w_in, w_out):
    hidden, slope = gelu_pair(z_pre)
    w_out_grad = lax.dot_general(hidden, grad_y, CONTRACT_ROWS, preferred_element_type=jnp.float32).astype(jnp.bfloat16)
    grad_hidden = lax.dot_general(grad_y, w_out, CONTRACT_COLS, preferred_element_type=jnp.float32)
    grad_pre = (grad_hidden * slope).astype(jnp.bfloat16)
    w_in_grad = lax.dot_general(x_in, grad_pre, CONTRACT_ROWS, preferred_element_type=jnp.float32).astype(jnp.bfloat16)
    grad_x = (grad_y.astype(jnp.float32) + lax.dot_general(grad_pre, w_in, CONTRACT_COLS, preferred_element_type=jnp.float32)).astype(jnp.bfloat16)
    return w_out_grad, w_in_grad, grad_x


def reduce_grad(grad, group_size):
    row_count, col_count = grad.shape
    pieces = grad.reshape(group_size, row_count // group_size, col_count)
    received = lax.all_to_all(pieces, 'group', 0, 0)
    part_sum = jnp.sum(received, axis=0, dtype=jnp.float32)
    part_sum = lax.psum_scatter(part_sum, 'second', scatter_dimension=0, tiled=True)
    part_sum = lax.psum_scatter(part_sum, 'third', scatter_dimension=0, tiled=True)
    full_sum = lax.all_gather(part_sum, 'third', axis=0, tiled=True)
    full_sum = lax.all_gather(full_sum, 'second', axis=0, tiled=True)
    return lax.all_gather(full_sum, 'group', axis=0, tiled=True)


def solution(mesh):
    group_size = mesh.shape['group']

    def device_step(x_one, z_one, x_two, z_two, grad_out, w1_in, w1_out, w2_in, w2_out):
        w2o_grad, w2i_grad, dx_two = block_backward(x_two, z_two, grad_out, w2_in, w2_out)
        sum_w2o = reduce_grad(w2o_grad, group_size)
        sum_w2i = reduce_grad(w2i_grad, group_size)
        w1o_grad, w1i_grad, dx_one = block_backward(x_one, z_one, dx_two, w1_in, w1_out)
        sum_w1o = reduce_grad(w1o_grad, group_size)
        sum_w1i = reduce_grad(w1i_grad, group_size)
        return sum_w2o, sum_w2i, sum_w1o, sum_w1i, dx_one

    row_spec = P(AXES, None)
    repl_spec = P()
    return jax.shard_map(
        device_step,
        mesh=mesh,
        in_specs=(row_spec, row_spec, row_spec, row_spec, row_spec, repl_spec, repl_spec, repl_spec, repl_spec),
        out_specs=(repl_spec, repl_spec, repl_spec, repl_spec, row_spec),
        check_vma=False,
    )
```

profile of v0, /device:TPU:1, one launch (start us, length us, event | category | flops | bytes accessed | tf_op | source)
XLA Modules:
  0.0 3637.5 jit_solution(5695488363146005621)
XLA Ops:
  7.2 20.2 fusion
  27.4 16.8 fusion.16
  44.2 16.8 fusion.1
  61.0 14.4 convolution_convert_fusion
  75.3 8.5 all-to-all-start.3
  83.8 14.3 convolution_convert_fusion.1
  98.2 348.9 %all-to-all-done.3 = bf16[8,256,8192]{2,1,0:T(8,128)(2,1)} async-done(((bf16[8,256,8192]{2,1,0:T(8,128)(2,1)}), bf16[8,256,8192]{2,1,0:T(8,128)(2,1)}, u32[]{:S(2)}, u32[]{:S(2)}) %all-to-all-start.3) | async-done | bytes 33554464 | tf_op jit(solution)/shard_map/all_to_all | solution.py:35
  447.0 8.4 all-to-all-start.1
  455.4 14.4 convolution_convert_fusion.2
  469.8 348.8 %all-to-all-done.1 = bf16[8,256,8192]{2,1,0:T(8,128)(2,1)} async-done(((bf16[8,256,8192]{2,1,0:T(8,128)(2,1)}), bf16[8,256,8192]{2,1,0:T(8,128)(2,1)}, u32[]{:S(2)}, u32[]{:S(2)}) %all-to-all-start.1) | async-done | bytes 33554464 | tf_op jit(solution)/shard_map/all_to_all | solution.py:35
  818.6 8.1 all-to-all-start.2
  826.7 15.1 convert_reduce_fusion
  841.9 15.1 convert_reduce_fusion.2
  857.0 1.6 copy-done.6
  858.6 0.1 copy-done.8
  858.7 14.3 convolution_convert_fusion.3
  873.0 316.9 %all-to-all-done.2 = bf16[8,1024,2048]{2,1,0:T(8,128)(2,1)} async-done(((bf16[8,1024,2048]{2,1,0:T(8,128)(2,1)}), bf16[8,1024,2048]{2,1,0:T(8,128)(2,1)}, u32[]{:S(2)}, u32[]{:S(2)}) %all-to-all-start.2) | async-done | bytes 33554464 | tf_op jit(solution)/shard_map/all_to_all | solution.py:35
  1189.9 8.1 all-to-all-start
  1198.1 15.2 convert_reduce_fusion.1
  1213.3 347.9 %all-to-all-done = bf16[8,1024,2048]{2,1,0:T(8,128)(2,1)} async-done(((bf16[8,1024,2048]{2,1,0:T(8,128)(2,1)}), bf16[8,1024,2048]{2,1,0:T(8,128)(2,1)}, u32[]{:S(2)}, u32[]{:S(2)}) %all-to-all-start) | async-done | bytes 33554464 | tf_op jit(solution)/shard_map/all_to_all | solution.py:35
  1561.2 15.2 convert_reduce_fusion.3
  1576.5 0.5 reduce-scatter.23.cloned.1.call-update
  1577.1 0.5 reduce-scatter.15.cloned.1.call-update
  1577.7 0.7 reduce-scatter.19.cloned.1.call-update
  1578.4 79.6 %reduce-scatter.9.cloned.1.call-done = f32[256,2048]{1,0:T(8,128)} async-done(((f32[1024,2048]{1,0:T(8,128)}), f32[256,2048]{1,0:T(8,128)}) %reduce-scatter.9.cloned.1.call-update) | async-done | bytes 2097168 | tf_op jit(solution)/shard_map/reduce_scatter | solution.py:37
  1658.0 0.3 all-gather.31.cloned.1.call-start
  1658.3 31.6 reduce-scatter.23.cloned.1.call-done
  1690.0 31.7 reduce-scatter.15.cloned.1.call-done
  1721.8 31.9 reduce-scatter.19.cloned.1.call-done
  1753.7 31.9 reduce-scatter.11.cloned.1.call-done
  1785.6 31.9 all-gather.31.cloned.1.call-done
  1817.6 32.1 all-gather.19.cloned.1.call-done
  1849.8 32.2 all-gather.25.cloned.1.call-done
  1882.1 32.1 all-gather.13.cloned.1.call-done
  1914.2 84.8 %all-gather.33.cloned.1.call-done = f32[256,8192]{1,0:T(8,128)} async-done(((f32[64,8192]{1,0:T(8,128)}), f32[256,8192]{1,0:T(8,128)}) %all-gather.33.cloned.1.call-update) | async-done | bytes 8388624 | tf_op jit(solution)/shard_map/all_gather | solution.py:40
  1999.1 85.7 %all-gather.21.cloned.1.call-done = f32[256,8192]{1,0:T(8,128)} async-done(((f32[64,8192]{1,0:T(8,128)}), f32[256,8192]{1,0:T(8,128)}) %all-gather.21.cloned.1.call-update) | async-done | bytes 8388624 | tf_op jit(solution)/shard_map/all_gather | solution.py:40
  2084.9 85.7 %all-gather.27.cloned.1.call-done = f32[1024,2048]{1,0:T(8,128)} async-done(((f32[256,2048]{1,0:T(8,128)}), f32[1024,2048]{1,0:T(8,128)}) %all-gather.27.cloned.1.call-update) | async-done | bytes 8388624 | tf_op jit(solution)/shard_map/all_gather | solution.py:40
  2170.7 85.7 %all-gather.15.cloned.1.call-done = f32[1024,2048]{1,0:T(8,128)} async-done(((f32[256,2048]{1,0:T(8,128)}), f32[1024,2048]{1,0:T(8,128)}) %all-gather.15.cloned.1.call-update) | async-done | bytes 8388624 | tf_op jit(solution)/shard_map/all_gather | solution.py:40
  2256.5 1.6 copy-done.3
  2258.0 16.8 fusion.17
  2274.8 282.1 %all-gather.35.cloned.1.call-done = f32[2048,8192]{1,0:T(8,128)} async-done(((f32[256,8192]{1,0:T(8,128)}), f32[2048,8192]{1,0:T(8,128)}) %all-gather.35.cloned.1.call-update) | async-done | bytes 67108880 | tf_op jit(solution)/shard_map/all_gather | solution.py:41
  2556.9 299.4 %all-gather.23.cloned.1.call-done = f32[2048,8192]{1,0:T(8,128)} async-done(((f32[256,8192]{1,0:T(8,128)}), f32[2048,8192]{1,0:T(8,128)}) %all-gather.23.cloned.1.call-update) | async-done | bytes 67108880 | tf_op jit(solution)/shard_map/all_gather | solution.py:41
  2856.3 299.5 %all-gather.29.cloned.1.call-done = f32[8192,2048]{1,0:T(8,128)} async-done(((f32[1024,2048]{1,0:T(8,128)}), f32[8192,2048]{1,0:T(8,128)}) %all-gather.29.cloned.1.call-update) | async-done | bytes 67108880 | tf_op jit(solution)/shard_map/all_gather | solution.py:41
  3155.8 299.4 %all-gather.17.cloned.1.call-done = f32[8192,2048]{1,0:T(8,128)} async-done(((f32[1024,2048]{1,0:T(8,128)}), f32[8192,2048]{1,0:T(8,128)}) %all-gather.17.cloned.1.call-update) | async-done | bytes 67108880 | tf_op jit(solution)/shard_map/all_gather | solution.py:41
  3455.2 43.8 %copy.18 = f32[8192,2048]{1,0:T(8,128)} copy(f32[8192,2048]{1,0:T(8,128)} %all-gather.17.cloned.1.call-done) | data formatting | bytes 134217728
  3499.0 44.2 %copy.19 = f32[2048,8192]{1,0:T(8,128)} copy(f32[2048,8192]{1,0:T(8,128)} %all-gather.23.cloned.1.call-done) | data formatting | bytes 134217728
  3543.1 43.6 %copy.20 = f32[8192,2048]{1,0:T(8,128)} copy(f32[8192,2048]{1,0:T(8,128)} %all-gather.29.cloned.1.call-done) | data formatting | bytes 134217728
  3586.7 44.0 %copy.21 = f32[2048,8192]{1,0:T(8,128)} copy(f32[2048,8192]{1,0:T(8,128)} %all-gather.35.cloned.1.call-done) | data formatting | bytes 134217728
  (56 shorter events, 1.0 us)
Async XLA Ops:
  7.2 53.8 %copy-start = (bf16[128,2048]{1,0:T(8,128)(2,1)S(1)}, bf16[128,2048]{1,0:T(8,128)(2,1)}, u32[]{:S(2)}) copy-start(bf16[128,2048]{1,0:T(8,128)(2,1)} %param.9) | copy-start | bytes 1572868
  7.2 20.2 copy-start.7
  61.0 14.4 copy-start.2
  75.3 8.5 copy-start.9
  75.3 371.7 %all-to-all-start.3 = ((bf16[8,256,8192]{2,1,0:T(8,128)(2,1)}), bf16[8,256,8192]{2,1,0:T(8,128)(2,1)}, u32[]{:S(2)}, u32[]{:S(2)}) async-start(bf16[8,256,8192]{2,1,0:T(8,128)(2,1)} %bitcast.25), calls=%async_computation.9 | async-start | bytes 67108864 | tf_op jit(solution)/shard_map/all_to_all | solution.py:35
  447.0 8.4 copy-start.4
  447.0 8.4 copy-start.5
  447.0 371.6 %all-to-all-start.1 = ((bf16[8,256,8192]{2,1,0:T(8,128)(2,1)}), bf16[8,256,8192]{2,1,0:T(8,128)(2,1)}, u32[]{:S(2)}, u32[]{:S(2)}) async-start(bf16[8,256,8192]{2,1,0:T(8,128)(2,1)} %bitcast.24), calls=%async_computation.3 | async-start | bytes 67108864 | tf_op jit(solution)/shard_map/all_to_all | solution.py:35
  818.6 371.3 %all-to-all-start.2 = ((bf16[8,1024,2048]{2,1,0:T(8,128)(2,1)}), bf16[8,1024,2048]{2,1,0:T(8,128)(2,1)}, u32[]{:S(2)}, u32[]{:S(2)}) async-start(bf16[8,1024,2048]{2,1,0:T(8,128)(2,1)} %bitcast.22), calls=%async_computation.6 | async-start | bytes 67108864 | tf_op jit(solution)/shard_map/all_to_all | solution.py:35
  826.7 749.8 %reduce-scatter.21.cloned.1.call-start = ((), (), s32[]{:S(2)}) async-start(), calls=%async_computation.27 | async-start | bytes 10485760 | tf_op jit(solution)/shard_map/reduce_scatter | solution.py:37
  841.9 735.3 %reduce-scatter.13.cloned.1.call-start = ((), (), s32[]{:S(2)}) async-start(), calls=%async_computation.17 | async-start | bytes 10485760 | tf_op jit(solution)/shard_map/reduce_scatter | solution.py:37
  857.0 1.6 copy-start.6
  857.0 1.7 copy-start.8
  1189.9 371.3 %all-to-all-start = ((bf16[8,1024,2048]{2,1,0:T(8,128)(2,1)}), bf16[8,1024,2048]{2,1,0:T(8,128)(2,1)}, u32[]{:S(2)}, u32[]{:S(2)}) async-start(bf16[8,1024,2048]{2,1,0:T(8,128)(2,1)} %bitcast.23), calls=%async_computation | async-start | bytes 67108864 | tf_op jit(solution)/shard_map/all_to_all | solution.py:35
  1198.1 379.6 %reduce-scatter.17.cloned.1.call-start = ((), (), s32[]{:S(2)}) async-start(), calls=%async_computation.22 | async-start | bytes 10485760 | tf_op jit(solution)/shard_map/reduce_scatter | solution.py:37
  1213.3 444.7 %reduce-scatter.9.cloned.1.call-start = ((), (), s32[]{:S(2)}) async-start(), calls=%async_computation.12 | async-start | bytes 10485760 | tf_op jit(solution)/shard_map/reduce_scatter | solution.py:37
  1576.5 113.5 %reduce-scatter.23.cloned.1.call-start = ((), (), s32[]{:S(2)}) async-start(), calls=%async_computation.28 | async-start | bytes 2621440 | tf_op jit(solution)/shard_map/reduce_scatter | solution.py:38
  1577.0 144.6 %reduce-scatter.15.cloned.1.call-start = ((), (), s32[]{:S(2)}) async-start(), calls=%async_computation.18 | async-start | bytes 2621440 | tf_op jit(solution)/shard_map/reduce_scatter | solution.py:38
  1577.6 176.0 %reduce-scatter.19.cloned.1.call-start = ((), (), s32[]{:S(2)}) async-start(), calls=%async_computation.23 | async-start | bytes 2621440 | tf_op jit(solution)/shard_map/reduce_scatter | solution.py:38
  1578.4 207.2 %reduce-scatter.11.cloned.1.call-start = ((), (), s32[]{:S(2)}) async-start(), calls=%async_computation.13 | async-start | bytes 2621440 | tf_op jit(solution)/shard_map/reduce_scatter | solution.py:38
  1658.0 159.6 %all-gather.31.cloned.1.call-start = ((), (), s32[]{:S(2)}) async-start(), calls=%async_computation.29 | async-start | bytes 2621440 | tf_op jit(solution)/shard_map/all_gather | solution.py:39
  1689.9 159.8 %all-gather.19.cloned.1.call-start = ((), (), s32[]{:S(2)}) async-start(), calls=%async_computation.19 | async-start | bytes 2621440 | tf_op jit(solution)/shard_map/all_gather | solution.py:39
  1721.7 160.3 %all-gather.25.cloned.1.call-start = ((), (), s32[]{:S(2)}) async-start(), calls=%async_computation.24 | async-start | bytes 2621440 | tf_op jit(solution)/shard_map/all_gather | solution.py:39
  1753.6 160.5 %all-gather.13.cloned.1.call-start = ((), (), s32[]{:S(2)}) async-start(), calls=%async_computation.14 | async-start | bytes 2621440 | tf_op jit(solution)/shard_map/all_gather | solution.py:39
  1785.6 213.5 %all-gather.33.cloned.1.call-start = ((), (), s32[]{:S(2)}) async-start(), calls=%async_computation.30 | async-start | bytes 10485760 | tf_op jit(solution)/shard_map/all_gather | solution.py:40
  1817.6 267.3 %all-gather.21.cloned.1.call-start = ((), (), s32[]{:S(2)}) async-start(), calls=%async_computation.20 | async-start | bytes 10485760 | tf_op jit(solution)/shard_map/all_gather | solution.py:40
  1849.7 320.9 %all-gather.27.cloned.1.call-start = ((), (), s32[]{:S(2)}) async-start(), calls=%async_computation.25 | async-start | bytes 10485760 | tf_op jit(solution)/shard_map/all_gather | solution.py:40
  1882.0 374.4 %all-gather.15.cloned.1.call-start = ((), (), s32[]{:S(2)}) async-start(), calls=%async_computation.15 | async-start | bytes 10485760 | tf_op jit(solution)/shard_map/all_gather | solution.py:40
  1914.2 642.7 %all-gather.35.cloned.1.call-start = ((), (), s32[]{:S(2)}) async-start(), calls=%async_computation.31 | async-start | bytes 75497472 | tf_op jit(solution)/shard_map/all_gather | solution.py:41
  1999.1 857.2 %all-gather.23.cloned.1.call-start = ((), (), s32[]{:S(2)}) async-start(), calls=%async_computation.21 | async-start | bytes 75497472 | tf_op jit(solution)/shard_map/all_gather | solution.py:41
  2084.9 1070.9 %all-gather.29.cloned.1.call-start = ((), (), s32[]{:S(2)}) async-start(), calls=%async_computation.26 | async-start | bytes 75497472 | tf_op jit(solution)/shard_map/all_gather | solution.py:41
  2170.7 1284.5 %all-gather.17.cloned.1.call-start = ((), (), s32[]{:S(2)}) async-start(), calls=%async_computation.16 | async-start | bytes 75497472 | tf_op jit(solution)/shard_map/all_gather | solution.py:41
  2256.4 1.6 copy-start.3
  3586.7 44.0 %copy-start.1 = (bf16[128,2048]{1,0:T(8,128)(2,1)S(1)}, bf16[128,2048]{1,0:T(8,128)(2,1)}, u32[]{:S(2)}) copy-start(bf16[128,2048]{1,0:T(8,128)(2,1)} %param.9) | copy-start | bytes 1572868
Sparse Core Ops, SparseCore 0:
  842.0 82.6 reduce-scatter.20
  927.7 80.2 reduce-scatter.12
  1213.4 82.6 reduce-scatter.16
  1576.6 81.3 reduce-scatter.8
  1660.2 29.6 reduce-scatter.22
  1692.2 29.4 reduce-scatter.14
  1724.1 29.4 reduce-scatter.18
  1756.0 29.4 reduce-scatter.10
  1787.2 30.2 all-gather.30
  1819.1 30.5 all-gather.18
  1851.4 30.5 all-gather.24
  1883.5 30.5 all-gather.12
  1915.8 83.1 all-gather.32
  2000.6 84.2 all-gather.20
  2086.4 84.2 all-gather.26
  2172.2 84.2 all-gather.14
  2258.0 298.8 all-gather.34
  2558.5 297.7 all-gather.22
  2858.0 297.7 all-gather.28
  3157.4 297.7 all-gather.16
where the time goes:
time: 3640 us
  waiting for transfers between devices  3220 us (88%)
  local copies, waits for them, and re-layouts  179 us (5%)
  matrix products  128 us (4%)
  other arithmetic  60.6 us (2%)
    all_to_all x4, waiting for transfers between devices, reduce_grad(): received = lax.all_to_all(pieces, 'group', 0, 0)  1360 us
    all_gather x4, waiting for transfers between devices, reduce_grad(): return lax.all_gather(full_sum, 'group', axis=0, tiled=True)  1180 us
    all_gather x4, waiting for transfers between devices, reduce_grad(): full_sum = lax.all_gather(full_sum, 'second', axis=0, tiled=True)  342 us
    unnamed x24, local copies, waits for them, and re-layouts  179 us
    all_gather x4, waiting for transfers between devices, reduce_grad(): full_sum = lax.all_gather(part_sum, 'third', axis=0, tiled=True)  128 us
    reduce_scatter x4, waiting for transfers between devices, reduce_grad(): lax.psum_scatter(part_sum, 'third', scatter_dimension=0, tiled=True)  127 us
    reduce_scatter x4, waiting for transfers between devices, reduce_grad(): lax.psum_scatter(part_sum, 'second', scatter_dimension=0, tiled=True)  79.6 us
  transfers between devices with their start and end apart: 24, of which 21 were waited for; matrix products, arithmetic and copies ran while one was open for 3% of the time, Pallas kernels for 0%

commit v1 on v0

v1 whole, which is shorter than its diff:
```python
import functools
import math
import jax
import jax.numpy as jnp
from jax import lax
from jax.experimental import pallas as pl
from jax.experimental.pallas import tpu as pltpu
from jax.sharding import PartitionSpec as P

AXES = ('third', 'second', 'group')
INV_ROOT_TWO = math.sqrt(0.5)
INV_ROOT_TWO_PI = 1.0 / math.sqrt(2.0 * math.pi)
CONTRACT_ROWS = (((0,), (0,)), ((), ()))
CONTRACT_COLS = (((1,), (1,)), ((), ()))


def gelu_pair(z_pre):
    z_val = z_pre.astype(jnp.float32)
    cdf_val = 0.5 * (1.0 + lax.erf(z_val * INV_ROOT_TWO))
    hidden = (z_val * cdf_val).astype(jnp.bfloat16)
    slope = cdf_val + z_val * jnp.exp(-0.5 * z_val * z_val) * INV_ROOT_TWO_PI
    return hidden, slope


def block_factors(z_pre, grad_y, w_in, w_out):
    hidden, slope = gelu_pair(z_pre)
    grad_hidden = lax.dot_general(grad_y, w_out, CONTRACT_COLS, preferred_element_type=jnp.float32)
    grad_pre = (grad_hidden * slope).astype(jnp.bfloat16)
    grad_x = (grad_y.astype(jnp.float32) + lax.dot_general(grad_pre, w_in, CONTRACT_COLS, preferred_element_type=jnp.float32)).astype(jnp.bfloat16)
    return hidden, grad_pre, grad_x


def rounded_sum(lhs_ref, rhs_ref, lhs_cols, rhs_cols):
    total = None
    for dev in range(lhs_ref.shape[0]):
        prod = lax.dot_general(lhs_ref[dev, :, lhs_cols], rhs_ref[dev, :, rhs_cols], CONTRACT_ROWS, preferred_element_type=jnp.float32)
        prod = prod.astype(jnp.bfloat16).astype(jnp.float32)
        total = prod if total is None else total + prod
    return total


def out_kernel(wide_ref, narrow_ref, part_ref):
    def body(step, carry):
        rows = pl.ds(pl.multiple_of(step * 128, 128), 128)
        tile = rounded_sum(wide_ref, narrow_ref, rows, slice(None))
        part_ref[pl.ds(step * 2, 2), 0] = tile.reshape(2, 64, tile.shape[-1])
        return carry
    lax.fori_loop(0, wide_ref.shape[-1] // 128, body, 0)


def in_kernel(narrow_ref, wide_ref, part_ref):
    part_ref[...] = rounded_sum(narrow_ref, wide_ref, slice(None), slice(None))


def partial_out(wide, narrow):
    devs, rows, width = wide.shape
    tile = 256
    per = 1024 // tile
    return pl.pallas_call(
        out_kernel,
        grid=(2 * per,),
        in_specs=[pl.BlockSpec((devs, rows, width), lambda i: (0, 0, 0)),
                  pl.BlockSpec((devs, rows, tile), lambda i: (0, 0, i))],
        out_specs=pl.BlockSpec((16, 1, 64, tile), lambda i: (0, i // per, 0, i % per)),
        out_shape=jax.ShapeDtypeStruct((16, 2, 64, 1024), jnp.float32),
        cost_estimate=pl.CostEstimate(flops=2 * devs * rows * width * 2048, bytes_accessed=16 << 20, transcendentals=0),
        name='partial_out',
    )(wide, narrow).reshape(2048, 1024)


def partial_in(narrow, wide):
    devs, rows, width = wide.shape
    tile = 128
    return pl.pallas_call(
        in_kernel,
        grid=(2048 // tile,),
        in_specs=[pl.BlockSpec((devs, rows, tile), lambda i: (0, 0, i)),
                  pl.BlockSpec((devs, rows, width), lambda i: (0, 0, 0))],
        out_specs=pl.BlockSpec((tile, width), lambda i: (i, 0)),
        out_shape=jax.ShapeDtypeStruct((2048, 1024), jnp.float32),
        cost_estimate=pl.CostEstimate(flops=2 * devs * rows * width * 2048, bytes_accessed=16 << 20, transcendentals=0),
        name='partial_in',
    )(narrow, wide)


def place_out_kernel(in_ref, out_ref):
    for g in range(8):
        out_ref[g, 0, :, :1024] = in_ref[0, g, 0, :64, :]
        out_ref[g, 0, :, 1024:] = in_ref[0, g, 0, 64:, :]


def place_in_kernel(in_ref, out_ref):
    for g in range(8):
        out_ref[:, g * 1024:(g + 1) * 1024] = in_ref[0, g, 0]


def place(gathered, index, transposed):
    cost = pl.CostEstimate(flops=1 << 30, bytes_accessed=128 << 20, transcendentals=0)
    in_spec = pl.BlockSpec((1, 8, 1, 128, 1024), lambda i: (i, 0, index, 0, 0))
    if transposed:
        return pl.pallas_call(
            place_in_kernel, grid=(16,), in_specs=[in_spec],
            out_specs=pl.BlockSpec((128, 8192), lambda i: (i, 0)),
            out_shape=jax.ShapeDtypeStruct((2048, 8192), jnp.float32),
            cost_estimate=cost, name='place_in',
        )(gathered)
    return pl.pallas_call(
        place_out_kernel, grid=(16,), in_specs=[in_spec],
        out_specs=pl.BlockSpec((8, 1, 64, 2048), lambda i: (0, i, 0, 0)),
        out_shape=jax.ShapeDtypeStruct((8, 16, 64, 2048), jnp.float32),
        cost_estimate=cost, name='place_out',
    )(gathered).reshape(8192, 2048)


def exchange_wide(arr):
    rows, cols = arr.shape
    return lax.all_to_all(arr.reshape(rows, 8, cols // 8).transpose(1, 0, 2), 'group', 0, 0)


def solution(mesh):
    def device_step(x_one, z_one, x_two, z_two, grad_out, w1_in, w1_out, w2_in, w2_out):
        hid_two, dz_two, dx_two = block_factors(z_two, grad_out, w2_in, w2_out)
        hid_one, dz_one, dx_one = block_factors(z_one, dx_two, w1_in, w1_out)
        narrow = lax.all_gather(jnp.concatenate([grad_out, x_two, x_one], axis=1), 'group', axis=0)
        dy_two_all, x_two_all, x_one_all = narrow[..., :2048], narrow[..., 2048:4096], narrow[..., 4096:]
        dx_two_all = lax.all_gather(dx_two, 'group', axis=0)
        parts = [
            partial_out(exchange_wide(hid_two), dy_two_all),
            partial_in(x_two_all, exchange_wide(dz_two)),
            partial_out(exchange_wide(hid_one), dx_two_all),
            partial_in(x_one_all, exchange_wide(dz_one)),
        ]
        def gather(mine):
            whole = lax.all_gather(mine, AXES, axis=0)
            return whole.reshape(16, 8, mine.shape[0], 128, 1024)

        def rs(part):
            return lax.psum_scatter(part, ('third', 'second'), scatter_dimension=0, tiled=True)
        mine = [rs(part) for part in parts]
        first = gather(jnp.stack(mine[1:]))
        held, first = lax.optimization_barrier((mine[0], first))
        last = gather(held[None])
        return (place(last, 0, False), place(first, 0, True), place(first, 1, False), place(first, 2, True), dx_one)

    row_spec = P(AXES, None)
    repl_spec = P()
    return jax.shard_map(
        device_step, mesh=mesh,
        in_specs=(row_spec,) * 5 + (repl_spec,) * 4,
        out_specs=(repl_spec,) * 4 + (row_spec,),
        check_vma=False,
    )
```

time: 3640 us -> 1170 us (0.32)
  waiting for transfers between devices: 3220 us -> 656 us
  Pallas kernels: 0 us -> 264 us
  local copies, waits for them, and re-layouts: 179 us -> 38.2 us
  blocking collectives: 0 us -> 108 us
  matrix products: 128 us -> 71.2 us
  other arithmetic: 60.6 us -> 10.1 us
    all_to_all x4 -> x1, waiting for transfers between devices: 1360 us -> 0.01 us  [exchange_wide(): lax.all_to_all(arr.reshape(rows, 8, cols // 8).transpose(1, 0, 2), 'group...]
    all_gather x12 -> x4, waiting for transfers between devices: 1650 us -> 455 us  [the longest x2 423 us: gather(): whole = lax.all_gather(mine, AXES, axis=0)]
    pallas_call x0 -> x8, Pallas kernels: none -> 264 us  [the longest x2 89.4 us: place(): pl.pallas_call(place_out_kernel, grid=(16,), in_specs=[in_spec], out_spec...]
    unnamed x24 -> x10, local copies, waits for them, and re-layouts: 179 us -> 1.04 us
    all_to_all x0 -> x3, blocking collectives: none -> 108 us  [exchange_wide(): lax.all_to_all(arr.reshape(rows, 8, cols // 8).transpose(1, 0, 2), 'group...]
    reduce_sum x4 -> x0, other arithmetic: 60.6 us -> none  [reduce_grad(): part_sum = jnp.sum(received, axis=0, dtype=jnp.float32)]
    dot_general x8 -> x4, matrix products: 128 us -> 71.2 us  [the longest x2 36.9 us: block_factors(): lax.dot_general(grad_y, w_out, CONTRACT_COLS, preferred_element_type=jnp....]
    reduce_scatter x8 -> x4, waiting for transfers between devices: 207 us -> 201 us  [rs(): lax.psum_scatter(part, ('third', 'second'), scatter_dimension=0, tiled=True)]
  transfers between devices with their start and end apart: 24 -> 9, of which waited for: 21 -> 7; matrix products, arithmetic and copies ran while one was open for 3% -> 7% of each run, Pallas kernels for 0% -> 19%
where the time goes in v1:
time: 1170 us
  waiting for transfers between devices  656 us (56%)
  Pallas kernels  264 us (23%)
  blocking collectives  108 us (9%)
  matrix products  71.2 us (6%)
  local copies, waits for them, and re-layouts  38.2 us (3%)
  between operations  14.2 us (1%)
    all_gather x2, waiting for transfers between devices, gather(): whole = lax.all_gather(mine, AXES, axis=0)  423 us
    reduce_scatter x4, waiting for transfers between devices, rs(): lax.psum_scatter(part, ('third', 'second'), scatter_dimension=0, tiled=True)  201 us
    all_to_all x3, blocking collectives, exchange_wide(): lax.all_to_all(arr.reshape(rows, 8, cols // 8).transpose(1, 0, 2), 'group...  108 us
    pallas_call x2, Pallas kernels, place(): pl.pallas_call(place_out_kernel, grid=(16,), in_specs=[in_spec], out_spec...  89.4 us
    pallas_call x2, Pallas kernels, place(): pl.pallas_call(place_in_kernel, grid=(16,), in_specs=[in_spec], out_specs...  89.4 us
    pallas_call x2, Pallas kernels, partial_out(): pl.pallas_call(out_kernel, grid=(2 * per,), in_specs=[pl.BlockSpec((devs,...  50.6 us
    dot_general x2, matrix products, block_factors(): lax.dot_general(grad_y, w_out, CONTRACT_COLS, preferred_element_type=jnp....  36.9 us
    pallas_call x2, Pallas kernels, partial_in(): pl.pallas_call(in_kernel, grid=(2048 // tile,), in_specs=[pl.BlockSpec((d...  34.8 us
  transfers between devices with their start and end apart: 9, of which 7 were waited for; matrix products, arithmetic and copies ran while one was open for 7% of the time, Pallas kernels for 19%

profile of v1, /device:TPU:1, one launch (start us, length us, event | category | flops | bytes accessed | tf_op | source)
XLA Modules:
  0.0 1166.4 jit_solution(14420928172558718567)
XLA Ops:
  7.2 0.0 all-gather.11.cloned.1.call-start
  7.2 20.2 %fusion = bf16[128,8192]{1,0:T(8,128)(2,1)S(1)} fusion(bf16[128,2048]{1,0:T(8,128)(2,1)} %param.13, bf16[8192,2048]{1,0:T(8,128)(2,1)} %param.17, bf16[128,8192]{1,0:T(8,128)(2,1)} %param.12), kind=kOutput, calls=%fused_computation.2 | convolution fusion | flops 4306501632 | bytes 38273024 | tf_op jit(solution)/shard_map/dot_general | solution.py:27
  27.5 17.5 %fusion.16 = bf16[128,2048]{1,0:T(8,128)(2,1)} fusion(bf16[128,8192]{1,0:T(8,128)(2,1)S(1)} %fusion, bf16[2048,8192]{1,0:T(8,128)(2,1)} %param.16, bf16[128,2048]{1,0:T(8,128)(2,1)S(1)} %copy-done.2), kind=kOutput, calls=%fused_computation.30 | convolution fusion | flops 4295753728 | bytes 36700160 | tf_op jit(solution)/shard_map/dot_general | solution.py:29
  45.0 0.0 all-gather.11.cloned.1.call-update
  45.1 0.0 all-gather.9.cloned.1.call-start
  45.1 2.4 pad_maximum_fusion
  47.6 0.0 all-gather.9.cloned.1.call-update
  47.6 0.0 reduce-scatter.9.cloned.1.call-start
  47.6 1.9 fusion.12
  49.5 3.2 copy.26
  52.8 2.6 copy.27
  55.4 46.3 %all_to_all.20.wide_ref = bf16[8,128,1024]{2,1,0:T(8,128)(2,1)} all-to-all(bf16[8,128,1024]{2,1,0:T(8,128)(2,1)} %bitcast.32), channel_id=1, replica_groups=mesh['third'=4,'second'=4,'group'=8] {'group'}, dimensions={0} | all-to-all | bytes 4194304 | tf_op jit(solution)/shard_map/all_to_all | solution.py:117
  101.6 0.4 all-gather.11.cloned.1.call-done
  102.1 25.3 %partial_out.3 = f32[16,2,64,1024]{3,2,1,0:T(8,128)} custom-call(bf16[8,128,1024]{2,1,0:T(8,128)(2,1)} %all_to_all.20.wide_ref, bf16[8,128,2048]{2,1,0:T(8,128)(2,1)} %bitcast.41), custom_call_target="tpu_custom_call" | custom-call | flops 4294967296 | bytes 16777216 | tf_op jit(solution)/shard_map/partial_out/pallas_call | solution.py:59
  127.4 1.0 copy-done.1
  128.4 16.7 %fusion.1 = bf16[128,8192]{1,0:T(8,128)(2,1)S(1)} fusion(bf16[128,2048]{1,0:T(8,128)(2,1)S(1)} %copy-done.1, bf16[8192,2048]{1,0:T(8,128)(2,1)} %param.15, bf16[128,8192]{1,0:T(8,128)(2,1)} %param.10), kind=kOutput, calls=%fused_computation.3 | convolution fusion | flops 4306501632 | bytes 38273024 | tf_op jit(solution)/shard_map/dot_general | solution.py:27
  145.1 2.4 copy.28
  147.5 3.9 copy.29
  151.4 4.5 all-to-all-start.3
  155.9 0.0 reduce-scatter.11.cloned.1.call-start
  156.0 30.9 %all-gather.9.cloned.1.call-done = bf16[1024,6144]{1,0:T(8,128)(2,1)} async-done(((bf16[128,6144]{1,0:T(8,128)(2,1)}), bf16[1024,6144]{1,0:T(8,128)(2,1)}) %all-gather.9.cloned.1.call-update) | async-done | bytes 12582928 | tf_op jit(solution)/shard_map/all_gather | solution.py:124
  186.9 9.0 fusion.18
  195.9 17.4 %partial_in.3 = f32[2048,1024]{1,0:T(8,128)} custom-call(bf16[8,128,2048]{2,1,0:T(8,128)(2,1)} %get-tuple-element.10.narrow_ref, bf16[8,128,1024]{2,1,0:T(8,128)(2,1)} %all-to-all-done.3.wide_ref), custom_call_target="tpu_custom_call" | custom-call | flops 4294967296 | bytes 16777216 | tf_op jit(solution)/shard_map/partial_in/pallas_call | solution.py:74
  213.3 0.0 reduce-scatter.7.cloned.1.call-start
  213.4 4.1 copy.24
  217.4 3.9 copy.25
  221.4 30.4 %all_to_all.21.wide_ref = bf16[8,128,1024]{2,1,0:T(8,128)(2,1)} all-to-all(bf16[8,128,1024]{2,1,0:T(8,128)(2,1)} %bitcast.34), channel_id=1, replica_groups=mesh['third'=4,'second'=4,'group'=8] {'group'}, dimensions={0} | all-to-all | bytes 4194304 | tf_op jit(solution)/shard_map/all_to_all | solution.py:117
  251.8 17.4 %partial_in.2 = f32[2048,1024]{1,0:T(8,128)} custom-call(bf16[8,128,2048]{2,1,0:T(8,128)(2,1)} %get-tuple-element.9.narrow_ref, bf16[8,128,1024]{2,1,0:T(8,128)(2,1)} %all_to_all.21.wide_ref), custom_call_target="tpu_custom_call" | custom-call | flops 4294967296 | bytes 16777216 | tf_op jit(solution)/shard_map/partial_in/pallas_call | solution.py:74
  269.2 0.0 reduce-scatter.5.cloned.1.call-start
  269.3 3.1 fusion.5
  272.4 4.1 copy.22
  276.5 3.9 copy.23
  280.4 31.3 %all_to_all.22.wide_ref = bf16[8,128,1024]{2,1,0:T(8,128)(2,1)} all-to-all(bf16[8,128,1024]{2,1,0:T(8,128)(2,1)} %bitcast.36), channel_id=1, replica_groups=mesh['third'=4,'second'=4,'group'=8] {'group'}, dimensions={0} | all-to-all | bytes 4194304 | tf_op jit(solution)/shard_map/all_to_all | solution.py:117
  311.7 25.3 %partial_out.2 = f32[16,2,64,1024]{3,2,1,0:T(8,128)} custom-call(bf16[8,128,1024]{2,1,0:T(8,128)(2,1)} %all_to_all.22.wide_ref, bf16[8,128,2048]{2,1,0:T(8,128)(2,1)} %get-tuple-element.11.narrow_ref), custom_call_target="tpu_custom_call" | custom-call | flops 4294967296 | bytes 16777216 | tf_op jit(solution)/shard_map/partial_out/pallas_call | solution.py:59
  337.0 0.0 all-gather.13.cloned.1.call-start
  337.1 0.0 reduce-scatter.9.cloned.1.call-done
  337.1 26.2 %reduce-scatter.11.cloned.1.call-done = f32[128,1024]{1,0:T(8,128)} async-done(((f32[2048,1024]{1,0:T(8,128)}), f32[128,1024]{1,0:T(8,128)}) %reduce-scatter.11.cloned.1.call-update) | async-done | bytes 524304 | tf_op jit(solution)/shard_map/reduce_scatter | solution.py:138
  363.3 88.5 %reduce-scatter.7.cloned.1.call-done = f32[128,1024]{1,0:T(8,128)} async-done(((f32[2048,1024]{1,0:T(8,128)}), f32[128,1024]{1,0:T(8,128)}) %reduce-scatter.7.cloned.1.call-update) | async-done | bytes 524304 | tf_op jit(solution)/shard_map/reduce_scatter | solution.py:138
  451.9 2.7 pad_maximum_fusion.1
  454.6 0.0 all-gather.15.cloned.1.call-start
  454.6 85.9 %reduce-scatter.5.cloned.1.call-done = f32[128,1024]{1,0:T(8,128)} async-done(((f32[2048,1024]{1,0:T(8,128)}), f32[128,1024]{1,0:T(8,128)}) %reduce-scatter.5.cloned.1.call-update) | async-done | bytes 524304 | tf_op jit(solution)/shard_map/reduce_scatter | solution.py:138
  540.5 408.3 %all-gather.13.cloned.1.call-done = f32[384,128,1024]{2,1,0:T(8,128)} async-done(((f32[3,128,1024]{2,1,0:T(8,128)}), f32[384,128,1024]{2,1,0:T(8,128)}) %all-gather.13.cloned.1.call-update) | async-done | bytes 201326608 | tf_op jit(solution)/shard_map/all_gather | solution.py:134
  948.8 16.8 %fusion.17 = bf16[128,2048]{1,0:T(8,128)(2,1)} fusion(bf16[128,8192]{1,0:T(8,128)(2,1)S(1)} %fusion.1, bf16[2048,8192]{1,0:T(8,128)(2,1)} %param.14, bf16[128,2048]{1,0:T(8,128)(2,1)S(1)} %copy-done.1), kind=kOutput, calls=%fused_computation.31 | convolution fusion | flops 4295753728 | bytes 36700160 | tf_op jit(solution)/shard_map/dot_general | solution.py:29
  965.6 44.7 %place_out.3 = f32[8,16,64,2048]{3,2,1,0:T(8,128)} custom-call(f32[16,8,3,128,1024]{4,3,2,1,0:T(8,128)} %bitcast.15.in_ref), custom_call_target="tpu_custom_call" | custom-call | flops 1073741824 | bytes 134217728 | tf_op jit(solution)/shard_map/place_out/pallas_call | solution.py:107
  1010.3 44.7 %place_in.2 = f32[2048,8192]{1,0:T(8,128)} custom-call(f32[16,8,3,128,1024]{4,3,2,1,0:T(8,128)} %bitcast.15.in_ref), custom_call_target="tpu_custom_call" | custom-call | flops 1073741824 | bytes 134217728 | tf_op jit(solution)/shard_map/place_in/pallas_call | solution.py:101
  1055.1 44.7 %place_in.3 = f32[2048,8192]{1,0:T(8,128)} custom-call(f32[16,8,3,128,1024]{4,3,2,1,0:T(8,128)} %bitcast.15.in_ref), custom_call_target="tpu_custom_call" | custom-call | flops 1073741824 | bytes 134217728 | tf_op jit(solution)/shard_map/place_in/pallas_call | solution.py:101
  1099.8 15.1 %all-gather.15.cloned.1.call-done = f32[16384,1024]{1,0:T(8,128)} async-done(((f32[128,1024]{1,0:T(8,128)}), f32[16384,1024]{1,0:T(8,128)}) %all-gather.15.cloned.1.call-update) | async-done | bytes 67108880 | tf_op jit(solution)/shard_map/all_gather | solution.py:134
  1114.8 44.7 %place_out.2 = f32[8,16,64,2048]{3,2,1,0:T(8,128)} custom-call(f32[16,8,1,128,1024]{4,3,2,1,0:T(8,128)} %bitcast.16.in_ref), custom_call_target="tpu_custom_call" | custom-call | flops 1073741824 | bytes 134217728 | tf_op jit(solution)/shard_map/place_out/pallas_call | solution.py:107
  (16 shorter events, 0.1 us)
Async XLA Ops:
  7.2 20.3 %copy-start.2 = (bf16[128,2048]{1,0:T(8,128)(2,1)S(1)}, bf16[128,2048]{1,0:T(8,128)(2,1)}, u32[]{:S(2)}) copy-start(bf16[128,2048]{1,0:T(8,128)(2,1)} %param.13) | copy-start | bytes 1572868
  7.2 94.9 %all-gather.11.cloned.1.call-start = ((), (), s32[]{:S(2)}) async-start(), calls=%async_computation.13 | async-start | bytes 4718592 | tf_op jit(solution)/shard_map/all_gather | solution.py:126
  27.5 17.6 %copy-start = (bf16[128,8192]{1,0:T(8,128)(2,1)}, bf16[128,8192]{1,0:T(8,128)(2,1)S(1)}, u32[]{:S(2)}) copy-start(bf16[128,8192]{1,0:T(8,128)(2,1)S(1)} %fusion) | copy-start | bytes 6291460
  27.5 17.6 %copy-start.4 = (bf16[128,2048]{1,0:T(8,128)(2,1)S(1)}, bf16[128,2048]{1,0:T(8,128)(2,1)}, u32[]{:S(2)}) copy-start(bf16[128,2048]{1,0:T(8,128)(2,1)} %param.9) | copy-start | bytes 1572868
  45.0 2.6 copy-start.3
  45.1 141.8 %all-gather.9.cloned.1.call-start = ((), (), s32[]{:S(2)}) async-start(), calls=%async_computation.12 | async-start | bytes 14155776 | tf_op jit(solution)/shard_map/all_gather | solution.py:124
  47.6 289.5 %reduce-scatter.9.cloned.1.call-start = ((), (), s32[]{:S(2)}) async-start(), calls=%async_computation.10 | async-start | bytes 8912896 | tf_op jit(solution)/shard_map/reduce_scatter | solution.py:138
  127.4 1.0 copy-start.1
  151.4 44.5 %all-to-all-start.3 = ((bf16[8,128,1024]{2,1,0:T(8,128)(2,1)}), bf16[8,128,1024]{2,1,0:T(8,128)(2,1)}, u32[]{:S(2)}, u32[]{:S(2)}) async-start(bf16[8,128,1024]{2,1,0:T(8,128)(2,1)} %bitcast.30), calls=%async_computation.6 | async-start | bytes 4194304 | tf_op jit(solution)/shard_map/all_to_all | solution.py:117
  155.9 207.4 %reduce-scatter.11.cloned.1.call-start = ((), (), s32[]{:S(2)}) async-start(), calls=%async_computation.11 | async-start | bytes 8912896 | tf_op jit(solution)/shard_map/reduce_scatter | solution.py:138
  213.3 238.6 %reduce-scatter.7.cloned.1.call-start = ((), (), s32[]{:S(2)}) async-start(), calls=%async_computation.9 | async-start | bytes 8912896 | tf_op jit(solution)/shard_map/reduce_scatter | solution.py:138
  269.2 271.3 %reduce-scatter.5.cloned.1.call-start = ((), (), s32[]{:S(2)}) async-start(), calls=%async_computation.8 | async-start | bytes 8912896 | tf_op jit(solution)/shard_map/reduce_scatter | solution.py:138
  337.0 611.8 %all-gather.13.cloned.1.call-start = ((), (), s32[]{:S(2)}) async-start(), calls=%async_computation.14 | async-start | bytes 202899456 | tf_op jit(solution)/shard_map/all_gather | solution.py:134
  454.6 660.2 %all-gather.15.cloned.1.call-start = ((), (), s32[]{:S(2)}) async-start(), calls=%async_computation.15 | async-start | bytes 67633152 | tf_op jit(solution)/shard_map/all_gather | solution.py:134
Sparse Core Ops, SparseCore 0:
  45.2 56.8 all-gather.10
  104.3 82.5 all-gather.8
  190.9 83.8 reduce-scatter.8
  278.6 84.7 reduce-scatter.10
  367.2 84.6 reduce-scatter.6
  455.7 84.7 reduce-scatter.4
  544.2 404.5 all-gather.12
  951.9 162.8 all-gather.14

commit v2 on v0

v2 whole, which is shorter than its diff:
```python
import functools
import math
import jax
import jax.numpy as jnp
from jax import lax
from jax.experimental import pallas as pl
from jax.experimental.pallas import tpu as pltpu
from jax.sharding import PartitionSpec as P

AXES = ('third', 'second', 'group')
MESH = pl.DeviceIdType.MESH
INV_ROOT_TWO = math.sqrt(0.5)
INV_ROOT_TWO_PI = 1.0 / math.sqrt(2.0 * math.pi)
CONTRACT_ROWS = (((0,), (0,)), ((), ()))
CONTRACT_COLS = (((1,), (1,)), ((), ()))
ROLES = (('x', 'y', 'z'), ('y', 'z', 'x'), ('z', 'x', 'y'), ('x', 'y', 'z'))
HALF = 512
CHIPS = 4
LINE = 8
TOKENS = 128
WIDTH = 1024
NARROW = 2048
WIDE = 8192
BOTH = (0, 1)
SLOTS = 6
ORDER = tuple(zip(map(int, '0102130451023410652317647523647523467567'), map(int, '0010102002311134012240121233232344433444')))


def gelu(z_pre):
    z_val = z_pre.astype(jnp.float32)
    return (z_val * (0.5 * (1.0 + lax.erf(z_val * INV_ROOT_TWO)))).astype(jnp.bfloat16)


def slope_of(z_pre):
    z_val = z_pre.astype(jnp.float32)
    cdf_val = 0.5 * (1.0 + lax.erf(z_val * INV_ROOT_TWO))
    return cdf_val + z_val * jnp.exp(-0.5 * z_val * z_val) * INV_ROOT_TWO_PI


def reduce_kernel(hid_two, hid_one, z_two, z_one, grad_out, x_two, x_one, w2_out, w2_in, w1_out,
                  early_ref, late_ref, dz_out, dx_two, land_w, land_n,
                  stage_w, stage_n, part, got1, got2, got3, got4, dz_buf, dy_buf, dx_buf, z_buf,
                  xs_n, xr_n, xs_w, xr_w, stage_sem_w, stage_sem_n, rs_send, rs_recv, z_sem, put_sem):
    narrows = (grad_out, x_two, dx_two, x_one)

    def wide_piece(m, line, h):
        if m % 2:
            return dz_out.at[m // 2, 2 * line + h]
        return (hid_two, hid_one)[m // 2].at[:, pl.ds(pl.multiple_of(line * WIDTH + h * HALF, HALF), HALF)]

    def fetch_tile(which, t):
        slot = t % 2
        if which == 1:
            def columns(k, carry):
                pltpu.make_async_copy(w2_in.at[pl.ds(2 * t, 2), :, pl.ds(pl.multiple_of(k * NARROW, NARROW), NARROW)],
                                      stage_n.at[slot, pl.ds(2 * k, 2)], stage_sem_n.at[slot]).start()
                return carry
            lax.fori_loop(0, 4, columns, 0)
        else:
            pltpu.make_async_copy((w2_out, None, w1_out)[which].at[pl.ds(8 * t, 8)], stage_n.at[slot], stage_sem_n.at[slot]).start()
            z_pre = (z_two, None, z_one)[which]
            pltpu.make_async_copy(z_pre.at[:, pl.ds(pl.multiple_of(t * WIDTH, WIDTH), WIDTH)], z_buf.at[slot], z_sem.at[slot]).start()

    def tiles(which, body):
        def step(t, carry):
            slot = t % 2
            pltpu.make_async_copy(stage_n.at[slot], stage_n.at[slot], stage_sem_n.at[slot]).wait()
            if which != 1:
                pltpu.make_async_copy(z_buf.at[slot], z_buf.at[slot], z_sem.at[slot]).wait()
            body(t, slot)

            @pl.when(t < 6)
            def _():
                fetch_tile(which, t + 2)
            if which < 2:
                @pl.when(t >= 6)
                def _():
                    fetch_tile(which + 1, t - 6)
            return carry
        lax.fori_loop(0, 8, step, 0)

    def weights(slot, pair):
        return stage_n[slot, 2 * pair:2 * pair + 2].reshape(256, NARROW)

    def grad_pre(which, grad_ref):
        def body(t, slot):
            for pair in range(4):
                grad_hidden = lax.dot_general(grad_ref[...], weights(slot, pair), CONTRACT_COLS, preferred_element_type=jnp.float32)
                at = 256 * (pair % 2)
                slope = slope_of(z_buf[slot, :, 256 * pair:256 * pair + 256])
                dz_buf[2 * t + pair // 2, :, at:at + 256] = (grad_hidden * slope).astype(jnp.bfloat16)
        tiles(which, body)
        put = pltpu.make_async_copy(dz_buf, dz_out.at[which // 2], put_sem.at[0])
        put.start()
        put.wait()

    def grad_input():
        def body(t, slot):
            total = None
            for k in range(16):
                at = HALF * (k % CHIPS)
                prod = lax.dot_general(dz_buf[k], weights(slot, k // 4)[:, at:at + HALF], CONTRACT_COLS, preferred_element_type=jnp.float32)
                total = prod if total is None else total + prod
            cols = pl.ds(pl.multiple_of(t * 256, 256), 256)
            dx_buf[:, cols] = (dy_buf[:, cols].astype(jnp.float32) + total).astype(jnp.bfloat16)
        tiles(1, body)
        put = pltpu.make_async_copy(dx_buf, dx_two, put_sem.at[1])
        put.start()
        put.wait()

    fetch_tile(0, 0)
    fetch_tile(0, 1)
    get_dy = pltpu.make_async_copy(grad_out, dy_buf, put_sem.at[1])
    get_dy.start()
    z, y, g = lax.axis_index('third'), lax.axis_index('second'), lax.axis_index('group')
    x, c = g // 2, g % 2
    pos = {'x': x, 'y': y, 'z': z}

    def device(axis, off, core):
        at = dict(pos)
        at[axis] = (pos[axis] + off) % CHIPS
        return (at['z'], at['y'], 2 * at['x'] + core)

    barrier = pltpu.get_barrier_semaphore()
    peers = [device(axis, off, core) for axis in 'xyz' for off in (1, 2, 3) for core in BOTH] + [device('x', 0, 1 - c)]
    for peer in peers:
        pl.semaphore_signal(barrier, inc=1, device_id=peer, device_id_type=MESH)
    pl.semaphore_wait(barrier, len(peers))

    def line_index(m):
        return 2 * pos[ROLES[m][0]] + c

    def direct_narrow(m, off, core):
        return pltpu.make_async_remote_copy(
            src_ref=narrows[m], dst_ref=land_n.at[m, line_index(m)], send_sem=xs_n.at[m, off], recv_sem=xr_n.at[m, line_index(m)],
            device_id=device(ROLES[m][0], off, core), device_id_type=MESH)

    def relay_narrow(m, off):
        source = 2 * ((pos[ROLES[m][0]] + off) % CHIPS) + c
        return pltpu.make_async_remote_copy(
            src_ref=land_n.at[m, source], dst_ref=land_n.at[m, source], send_sem=xs_n.at[m, 3 + off], recv_sem=xr_n.at[m, source],
            device_id=device('x', 0, 1 - c), device_id_type=MESH)

    def wide_copy(m, h, off, core):
        me = line_index(m)
        target = 2 * ((pos[ROLES[m][0]] + off) % CHIPS) + core
        return pltpu.make_async_remote_copy(
            src_ref=wide_piece(m, target, h), dst_ref=land_w.at[m, h, me], send_sem=xs_w.at[m, h, 2 * off + core], recv_sem=xr_w.at[m, h, me],
            device_id=device(ROLES[m][0], off, core), device_id_type=MESH)

    def over_chips(fn):
        lax.fori_loop(1, 4, lambda off, carry: (fn(off), carry)[1], 0)

    def start_narrow(m):
        over_chips(lambda off: direct_narrow(m, off, c).start())
        direct_narrow(m, 0, 1 - c).start()

    def start_wide(m, h):
        def both(off):
            wide_copy(m, h, off, 0).start()
            wide_copy(m, h, off, 1).start()
        over_chips(both)
        wide_copy(m, h, 0, 1 - c).start()

    def relay(m):
        def one(off):
            source = 2 * ((pos[ROLES[m][0]] + off) % CHIPS) + c
            pltpu.make_async_copy(land_n.at[m, source], land_n.at[m, source], xr_n.at[m, source]).wait()
            relay_narrow(m, off).start()
        over_chips(one)

    def wait_exchange_sends(m):
        over_chips(lambda off: direct_narrow(m, off, c).wait_send())
        direct_narrow(m, 0, 1 - c).wait_send()
        over_chips(lambda off: relay_narrow(m, off).wait_send())
        for h in BOTH:
            def both(off):
                wide_copy(m, h, off, 0).wait_send()
                wide_copy(m, h, off, 1).wait_send()
            over_chips(both)
            wide_copy(m, h, 0, 1 - c).wait_send()

    def stage_narrow(m):
        me = line_index(m)
        slot = m % 2

        def other_core(off, carry):
            source = 2 * ((pos[ROLES[m][0]] + off) % CHIPS) + 1 - c
            pltpu.make_async_copy(land_n.at[m, source], land_n.at[m, source], xr_n.at[m, source]).wait()
            return carry
        lax.fori_loop(0, 4, other_core, 0)

        def fetch(off, carry):
            source = (me + off) % LINE
            pltpu.make_async_copy(land_n.at[m, source], stage_n.at[slot, source], stage_sem_n.at[slot]).start()
            return carry
        lax.fori_loop(1, LINE, fetch, 0)
        pltpu.make_async_copy(narrows[m], stage_n.at[slot, me], stage_sem_n.at[slot]).start()

    def stage_wide(m, h):
        me = line_index(m)

        def fetch(off, carry):
            source = (me + off) % LINE
            pltpu.make_async_copy(land_w.at[m, h, source], land_w.at[m, h, source], xr_w.at[m, h, source]).wait()
            pltpu.make_async_copy(land_w.at[m, h, source], stage_w.at[h, source], stage_sem_w.at[h]).start()
            return carry
        lax.fori_loop(1, LINE, fetch, 0)
        pltpu.make_async_copy(wide_piece(m, me, h), stage_w.at[h, me], stage_sem_w.at[h]).start()

    def rs_copy(j, color, stage, side):
        m, h = j // 2, j % 2
        first, second = ROLES[m][1:] if color == 0 else ROLES[m][:0:-1]
        p, q = pos[first], pos[second]
        slot, got = j % SLOTS, j % 6
        sign = 1 if side == 0 else 3
        mine = part.at[slot, color]
        if stage == 1:
            src, dst, axis = mine.at[(p + 2) % CHIPS, pl.ds(2 * side, 2)], got1.at[got, color, side], first
        elif stage == 2:
            src, dst, axis = mine.at[(p + sign) % CHIPS], got2.at[got, color, side], first
        elif stage == 3:
            src, dst, axis = mine.at[p, (q + 2) % CHIPS, pl.ds(32 * side, 32)], got3.at[got, color, side], second
        else:
            src, dst, axis = mine.at[p, (q + sign) % CHIPS], got4.at[got, color, side], second
        return pltpu.make_async_remote_copy(
            src_ref=src, dst_ref=dst, send_sem=rs_send.at[j, color, stage - 1, side], recv_sem=rs_recv.at[j, color, stage - 1, side],
            device_id=device(axis, sign, c), device_id_type=MESH)

    def compute(j):
        m, h = j // 2, j % 2
        slot = j % SLOTS
        a, b = pos[ROLES[m][1]], pos[ROLES[m][2]]
        if h == 0:
            pltpu.make_async_copy(stage_n.at[m % 2], stage_n.at[m % 2], stage_sem_n.at[m % 2]).wait()
        pltpu.make_async_copy(stage_w.at[h], stage_w.at[h], stage_sem_w.at[h]).wait()
        wide, narrow = stage_w.at[h], stage_n.at[m % 2]

        def piece(i, carry):
            k = jnp.maximum(i - 7, 0)
            pa = jnp.where(i < 4, a + 2, jnp.where(i < 7, a + i - 1, a + 3 + k // 3)) % CHIPS
            pb = jnp.where(i < 4, i, jnp.where(i < 7, b + 2, b + 3 + k % 3)) % CHIPS
            if m % 2 == 0:
                lhs, lhs_at, rhs, rhs_at = wide, pa * TOKENS, narrow, pb * HALF
            else:
                lhs, lhs_at, rhs, rhs_at = narrow, (pa * 4 + pb) * TOKENS, wide, 0
            lhs_cols = pl.ds(pl.multiple_of(lhs_at, TOKENS), TOKENS)
            rhs_cols = pl.ds(pl.multiple_of(rhs_at, HALF), HALF) if m % 2 == 0 else slice(None)
            total = None
            for dev in range(8):
                prod = lax.dot_general(lhs[dev, :, lhs_cols], rhs[dev, :, rhs_cols], CONTRACT_ROWS, preferred_element_type=jnp.float32)
                prod = prod.astype(jnp.bfloat16).astype(jnp.float32)
                total = prod if total is None else total + prod
            part[slot, 0, pa, pb] = total[:64]
            part[slot, 1, pb, pa] = total[64:]

            @pl.when(i == 3)
            def _():
                rs_copy(j, 0, 1, 0).start()
                rs_copy(j, 0, 1, 1).start()

            @pl.when(i == 6)
            def _():
                rs_copy(j, 1, 1, 0).start()
                rs_copy(j, 1, 1, 1).start()
            return carry
        lax.fori_loop(0, 16, piece, 0)

    def coords(j, color):
        m = j // 2
        first, second = ROLES[m][1:] if color == 0 else ROLES[m][:0:-1]
        return pos[first], pos[second]

    def stage_two(j):
        slot, got = j % SLOTS, j % 6
        for color in BOTH:
            p, q = coords(j, color)
            rs_copy(j, color, 1, 0).wait_recv()
            part[slot, color, (p + 1) % CHIPS, 0:2] += got1[got, color, 0]
            rs_copy(j, color, 1, 1).wait_recv()
            part[slot, color, (p + 3) % CHIPS, 2:4] += got1[got, color, 1]
            rs_copy(j, color, 2, 0).start()
            rs_copy(j, color, 2, 1).start()

    def stage_three(j):
        slot, got = j % SLOTS, j % 6
        for color in BOTH:
            p, q = coords(j, color)
            rs_copy(j, color, 2, 0).wait_recv()
            rs_copy(j, color, 2, 1).wait_recv()
            part[slot, color, p] += got2[got, color, 0] + got2[got, color, 1]
        for color in BOTH:
            rs_copy(j, color, 3, 0).start()
            rs_copy(j, color, 3, 1).start()

    def stage_four(j):
        slot, got = j % SLOTS, j % 6
        for color in BOTH:
            p, q = coords(j, color)
            rs_copy(j, color, 3, 0).wait_recv()
            part[slot, color, p, (q + 1) % CHIPS, 0:32] += got3[got, color, 0]
            rs_copy(j, color, 3, 1).wait_recv()
            part[slot, color, p, (q + 3) % CHIPS, 32:64] += got3[got, color, 1]
            rs_copy(j, color, 4, 0).start()
            rs_copy(j, color, 4, 1).start()

    def stage_five(j):
        m, h = j // 2, j % 2
        slot, got = j % SLOTS, j % 6
        for color in BOTH:
            p, q = coords(j, color)
            rs_copy(j, color, 4, 0).wait_recv()
            rs_copy(j, color, 4, 1).wait_recv()
            out_ref = late_ref.at[0] if m == 3 else early_ref.at[m]
            out_ref[64 * color:64 * color + 64, h * HALF:(h + 1) * HALF] = part[slot, color, p, q] + got4[got, color, 0] + got4[got, color, 1]

    def drain(j):
        for color in BOTH:
            for stage in (1, 2, 3, 4):
                for side in BOTH:
                    rs_copy(j, color, stage, side).wait_send()

    start_narrow(0)
    start_narrow(1)
    for h in BOTH:
        start_wide(0, h)
    for h in BOTH:
        start_wide(2, h)
    start_narrow(3)
    get_dy.wait()
    grad_pre(0, dy_buf)
    for h in BOTH:
        start_wide(1, h)
    grad_input()
    start_narrow(2)
    relay(0)
    relay(1)
    grad_pre(2, dx_buf)
    for h in BOTH:
        start_wide(3, h)
    stage_narrow(0)
    stage_wide(0, 0)

    def compute_step(j):
        if j == 6:
            relay(3)
            stage_narrow(3)
            stage_wide(3, 0)
        if j >= SLOTS:
            drain(j - SLOTS)
        if j + 1 < 8 and j + 1 != 6:
            if j + 1 == 4:
                relay(2)
            if (j + 1) % 2 == 0:
                stage_narrow((j + 1) // 2)
            stage_wide((j + 1) // 2, (j + 1) % 2)
        compute(j)

    steps = (compute_step, stage_two, stage_three, stage_four, stage_five)
    for job, stage in ORDER:
        steps[stage](job)
    for j in range(8 - SLOTS, 8):
        drain(j)
    for m in range(4):
        wait_exchange_sends(m)


def reduce_factors(*operands):
    f32, bf16, dma = jnp.float32, jnp.bfloat16, pltpu.SemaphoreType.DMA
    any_spec = pl.BlockSpec(memory_space=pl.ANY)
    vmem_spec = pl.BlockSpec(memory_space=pltpu.VMEM)
    return pl.pallas_call(
        reduce_kernel,
        out_shape=(jax.ShapeDtypeStruct((3, TOKENS, WIDTH), f32), jax.ShapeDtypeStruct((1, TOKENS, WIDTH), f32),
                   jax.ShapeDtypeStruct((2, 16, TOKENS, HALF), bf16), jax.ShapeDtypeStruct((TOKENS, NARROW), bf16),
                   jax.ShapeDtypeStruct((4, 2, 8, TOKENS, HALF), bf16), jax.ShapeDtypeStruct((4, 8, TOKENS, NARROW), bf16)),
        in_specs=[any_spec] * len(operands),
        out_specs=(vmem_spec, vmem_spec) + (any_spec,) * 4,
        scratch_shapes=[
            pltpu.VMEM((2, 8, TOKENS, HALF), bf16), pltpu.VMEM((2, 8, TOKENS, NARROW), bf16),
            pltpu.VMEM((SLOTS, 2, 4, 4, 64, HALF), f32),
            pltpu.VMEM((6, 2, 2, 2, 64, HALF), f32), pltpu.VMEM((6, 2, 2, 4, 64, HALF), f32),
            pltpu.VMEM((6, 2, 2, 32, HALF), f32), pltpu.VMEM((6, 2, 2, 64, HALF), f32),
            pltpu.VMEM((16, TOKENS, HALF), bf16), pltpu.VMEM((TOKENS, NARROW), bf16), pltpu.VMEM((TOKENS, NARROW), bf16), pltpu.VMEM((2, TOKENS, WIDTH), bf16),
            dma((4, 8)), dma((4, 8)), dma((4, 2, 8)), dma((4, 2, 8)), dma((2,)), dma((2,)),
            dma((8, 2, 4, 2)), dma((8, 2, 4, 2)), dma((2,)), dma((2,)),
        ],
        compiler_params=pltpu.CompilerParams(collective_id=0, has_side_effects=True, vmem_limit_bytes=67043328),
        cost_estimate=pl.CostEstimate(flops=1 << 34, bytes_accessed=64 << 20, transcendentals=0),
        name='reduce_factors',
    )(*operands)[:4]


def place_out_kernel(lead, in_ref, out_ref):
    for q in range(4):
        for core in BOTH:
            for h in BOTH:
                piece = in_ref[q, 0, 0, core, 0] if lead else in_ref[0, q, 0, core, 0]
                out_ref[core, h, 0, :, q * HALF:(q + 1) * HALF] = piece[:, h * HALF:(h + 1) * HALF]


def place_in_kernel(lead, in_ref, out_ref):
    for e in range(4):
        for core in BOTH:
            at = (2 * e + core) * WIDTH
            out_ref[:, at:at + WIDTH] = in_ref[0, e, 0, core, 0] if lead else in_ref[0, 0, e, core, 0]


def place(gathered, index, m):
    common = dict(grid=(4, 4), name='place', cost_estimate=pl.CostEstimate(flops=1 << 30, bytes_accessed=TOKENS << 20, transcendentals=0))
    f32 = jnp.float32
    if m == 0:
        return pl.pallas_call(
            functools.partial(place_out_kernel, True),
            in_specs=[pl.BlockSpec((4, 1, 1, 2, 1, TOKENS, WIDTH), lambda i, k: (0, i, k, 0, index, 0, 0))],
            out_specs=pl.BlockSpec((2, 2, 1, TOKENS, NARROW), lambda i, k: (k, 0, i, 0, 0)),
            out_shape=jax.ShapeDtypeStruct((8, 2, 4, TOKENS, NARROW), f32), **common)(gathered).reshape(WIDE, NARROW)
    if m == 2:
        return pl.pallas_call(
            functools.partial(place_out_kernel, False),
            in_specs=[pl.BlockSpec((1, 4, 1, 2, 1, TOKENS, WIDTH), lambda i, k: (k, 0, i, 0, index, 0, 0))],
            out_specs=pl.BlockSpec((2, 2, 1, TOKENS, NARROW), lambda i, k: (k, 0, i, 0, 0)),
            out_shape=jax.ShapeDtypeStruct((8, 2, 4, TOKENS, NARROW), f32), **common)(gathered).reshape(WIDE, NARROW)
    if m == 1:
        return pl.pallas_call(
            functools.partial(place_in_kernel, True),
            in_specs=[pl.BlockSpec((1, 4, 1, 2, 1, TOKENS, WIDTH), lambda i, k: (i, 0, k, 0, index, 0, 0))],
            out_specs=pl.BlockSpec((TOKENS, WIDE), lambda i, k: (4 * i + k, 0)),
            out_shape=jax.ShapeDtypeStruct((NARROW, WIDE), f32), **common)(gathered)
    return pl.pallas_call(
        functools.partial(place_in_kernel, False),
        in_specs=[pl.BlockSpec((1, 1, 4, 2, 1, TOKENS, WIDTH), lambda i, k: (k, i, 0, 0, index, 0, 0))],
        out_specs=pl.BlockSpec((TOKENS, WIDE), lambda i, k: (4 * i + k, 0)),
        out_shape=jax.ShapeDtypeStruct((NARROW, WIDE), f32), **common)(gathered)


def solution(mesh):
    def device_step(x_one, z_one, x_two, z_two, grad_out, w1_in, w1_out, w2_in, w2_out):
        early, late, grad_pre, dx_two = reduce_factors(
            gelu(z_two), gelu(z_one), z_two, z_one, grad_out, x_two, x_one,
            w2_out.reshape(64, TOKENS, NARROW), w2_in.reshape(16, TOKENS, WIDE), w1_out.reshape(64, TOKENS, NARROW))
        dz_one = grad_pre[1].transpose(1, 0, 2).reshape(TOKENS, WIDE)
        dx_one = (dx_two.astype(jnp.float32) + lax.dot_general(dz_one, w1_in, CONTRACT_COLS, preferred_element_type=jnp.float32)).astype(jnp.bfloat16)

        def gather(part):
            whole = lax.all_gather(part, AXES, axis=0)
            return whole.reshape(CHIPS, CHIPS, CHIPS, 2, part.shape[0], TOKENS, WIDTH)

        first = gather(early)
        held, first = lax.optimization_barrier((late, first))
        last = gather(held)
        return (place(first, 0, 0), place(first, 1, 1), place(first, 2, 2), place(last, 0, 3), dx_one)

    row_spec = P(AXES, None)
    repl_spec = P()
    return jax.shard_map(
        device_step, mesh=mesh,
        in_specs=(row_spec,) * 5 + (repl_spec,) * 4,
        out_specs=(repl_spec,) * 4 + (row_spec,),
        check_vma=False,
    )
```

time: 3640 us -> 833 us (0.23)
  waiting for transfers between devices: 3220 us -> 410 us
  Pallas kernels: 0 us -> 379 us
  local copies, waits for them, and re-layouts: 179 us -> 6.19 us
  matrix products: 128 us -> 17 us
  other arithmetic: 60.6 us -> 5.48 us
    all_to_all x4 -> x0, waiting for transfers between devices: 1360 us -> none  [reduce_grad(): received = lax.all_to_all(pieces, 'group', 0, 0)]
    all_gather x12 -> x2, waiting for transfers between devices: 1650 us -> 410 us  [gather(): whole = lax.all_gather(part, AXES, axis=0)]
    pallas_call x0 -> x5, Pallas kernels: none -> 379 us  [the longest x1 200 us: reduce_factors(): pl.pallas_call(reduce_kernel, out_shape=(jax.ShapeDtypeStruct((3, TOKENS,...]
    reduce_scatter x8 -> x0, waiting for transfers between devices: 207 us -> none  [the longest x4 127 us: reduce_grad(): lax.psum_scatter(part_sum, 'third', scatter_dimension=0, tiled=True)]
    unnamed x24 -> x2, local copies, waits for them, and re-layouts: 179 us -> 0.01 us
    dot_general x8 -> x1, matrix products: 128 us -> 17 us  [device_step(): lax.dot_general(dz_one, w1_in, CONTRACT_COLS, preferred_element_type=jnp....]
    reduce_sum x4 -> x0, other arithmetic: 60.6 us -> none  [reduce_grad(): part_sum = jnp.sum(received, axis=0, dtype=jnp.float32)]
  transfers between devices with their start and end apart: 24 -> 2, of which waited for: 21 -> 2; matrix products, arithmetic and copies ran while one was open for 3% -> 3% of each run, Pallas kernels for 0% -> 16%
where the time goes in v2:
time: 833 us; the launch traced here: 832 us
  waiting for transfers between devices  410 us (49%)
  Pallas kernels  379 us (45%)
  matrix products  17 us (2%)
  between operations  14.1 us (2%)
    all_gather x2, waiting for transfers between devices, gather(): whole = lax.all_gather(part, AXES, axis=0)  410 us
    pallas_call x1, Pallas kernels, reduce_factors(): pl.pallas_call(reduce_kernel, out_shape=(jax.ShapeDtypeStruct((3, TOKENS,...  200 us
    pallas_call x1, Pallas kernels, place(): pl.pallas_call(functools.partial(place_out_kernel, True), in_specs=[pl.Bl...  44.7 us
    pallas_call x1, Pallas kernels, place(): pl.pallas_call(functools.partial(place_out_kernel, False), in_specs=[pl.B...  44.7 us
    pallas_call x1, Pallas kernels, place(): pl.pallas_call(functools.partial(place_in_kernel, True), in_specs=[pl.Blo...  44.7 us
    pallas_call x1, Pallas kernels, place(): pl.pallas_call(functools.partial(place_in_kernel, False), in_specs=[pl.Bl...  44.7 us
    dot_general x1, matrix products, device_step(): lax.dot_general(dz_one, w1_in, CONTRACT_COLS, preferred_element_type=jnp....  17 us
  transfers between devices with their start and end apart: 2, of which 2 were waited for; matrix products, arithmetic and copies ran while one was open for 3% of the time, Pallas kernels for 16%

profile of v2, /device:TPU:1, one launch (start us, length us, event | category | flops | bytes accessed | tf_op | source)
XLA Modules:
  0.0 832.0 jit_solution(17114797125472244976)
XLA Ops:
  7.2 0.0 all-gather.5.cloned.1.call-start
  7.2 5.5 fusion.3
  12.7 199.8 %reduce_factors.1 = (f32[3,128,1024]{2,1,0:T(8,128)}, f32[1,128,1024]{2,1,0:T(8,128)}, bf16[2,16,128,512]{3,2,1,0:T(8,128)(2,1)}, bf16[128,2048]{1,0:T(8,128)(2,...) custom-call(bf16[128,8192]{1,0:T(8,128)(2,1)} %get-tuple-element.17.hid_two, ...), custom_call_target="tpu_custom_call" | custom-call | flops 17179869184 | bytes 67108864 | tf_op jit(solution)/shard_map/reduce_factors/pallas_call | solution.py:372
  212.5 0.0 all-gather.5.cloned.1.call-update
  212.5 0.2 all-gather.7.cloned.1.call-start
  212.8 401.6 %all-gather.5.cloned.1.call-done = f32[384,128,1024]{2,1,0:T(8,128)} async-done(((f32[3,128,1024]{2,1,0:T(8,128)}), f32[384,128,1024]{2,1,0:T(8,128)}) %all-gather.5.cloned.1.call-update) | async-done | bytes 201326608 | tf_op jit(solution)/shard_map/all_gather | solution.py:446
  614.4 0.0 all-gather.7.cloned.1.call-update
  614.4 0.0 copy-start
  614.4 3.2 slice_bitcast_fusion
  617.6 3.0 copy.15
  620.6 0.0 copy-done
  620.6 17.0 %fusion.8 = bf16[128,2048]{1,0:T(8,128)(2,1)} fusion(bf16[128,8192]{0,1:T(8,128)(2,1)S(1)} %bitcast.17, bf16[2048,8192]{1,0:T(8,128)(2,1)} %param.14, bf16[128,2048]{1,0:T(8,128)(2,1)S(1)} %copy-done), kind=kOutput, calls=%fused_computation.13 | convolution fusion | flops 4295753728 | bytes 36700160 | tf_op jit(solution)/shard_map/dot_general | solution.py:443
  637.6 44.7 %place.4 = f32[8,2,4,128,2048]{4,3,2,1,0:T(8,128)} custom-call(f32[4,4,4,2,3,128,1024]{6,5,4,3,2,1,0:T(8,128)} %bitcast.3.in_ref), custom_call_target="tpu_custom_call" | custom-call | flops 1073741824 | bytes 134217728 | tf_op jit(solution)/shard_map/place/pallas_call | solution.py:413
  682.3 44.7 %place.6 = f32[8,2,4,128,2048]{4,3,2,1,0:T(8,128)} custom-call(f32[4,4,4,2,3,128,1024]{6,5,4,3,2,1,0:T(8,128)} %bitcast.3.in_ref), custom_call_target="tpu_custom_call" | custom-call | flops 1073741824 | bytes 134217728 | tf_op jit(solution)/shard_map/place/pallas_call | solution.py:419
  727.1 44.7 %place.5 = f32[2048,8192]{1,0:T(8,128)} custom-call(f32[4,4,4,2,3,128,1024]{6,5,4,3,2,1,0:T(8,128)} %bitcast.3.in_ref), custom_call_target="tpu_custom_call" | custom-call | flops 1073741824 | bytes 134217728 | tf_op jit(solution)/shard_map/place/pallas_call | solution.py:425
  771.8 8.6 %all-gather.7.cloned.1.call-done = f32[128,128,1024]{2,1,0:T(8,128)} async-done(((f32[1,128,1024]{2,1,0:T(8,128)}), f32[128,128,1024]{2,1,0:T(8,128)}) %all-gather.7.cloned.1.call-update) | async-done | bytes 67108880 | tf_op jit(solution)/shard_map/all_gather | solution.py:446
  780.4 44.7 %place.7 = f32[2048,8192]{1,0:T(8,128)} custom-call(f32[4,4,4,2,1,128,1024]{6,5,4,3,2,1,0:T(8,128)} %bitcast.6.in_ref), custom_call_target="tpu_custom_call" | custom-call | flops 1073741824 | bytes 134217728 | tf_op jit(solution)/shard_map/place/pallas_call | solution.py:430
Async XLA Ops:
  7.2 607.2 %all-gather.5.cloned.1.call-start = ((), (), s32[]{:S(2)}) async-start(), calls=%async_computation | async-start | bytes 202899456 | tf_op jit(solution)/shard_map/all_gather | solution.py:446
  212.5 567.9 %all-gather.7.cloned.1.call-start = ((), (), s32[]{:S(2)}) async-start(), calls=%async_computation.1 | async-start | bytes 67633152 | tf_op jit(solution)/shard_map/all_gather | solution.py:446
  614.4 6.2 copy-start
Sparse Core Ops, SparseCore 0:
  212.6 401.7 all-gather.4
  617.5 162.8 all-gather.6

commit v3 on v2

v3 whole, which is shorter than its diff:
```python
import functools
import math
import jax
import jax.numpy as jnp
from jax import lax
from jax.experimental import pallas as pl
from jax.experimental.pallas import tpu as pltpu
from jax.sharding import PartitionSpec as P

AXES = ('third', 'second', 'group')
MESH = pl.DeviceIdType.MESH
INV_ROOT_TWO = math.sqrt(0.5)
INV_ROOT_TWO_PI = 1.0 / math.sqrt(2.0 * math.pi)
CONTRACT_ROWS = (((0,), (0,)), ((), ()))
CONTRACT_COLS = (((1,), (1,)), ((), ()))
ROLES = (('x', 'y', 'z'), ('y', 'z', 'x'), ('z', 'x', 'y'), ('x', 'y', 'z'))
GATHER = ('yzx', 'zxy', 'xyz')
HALF = 512
CHIPS = 4
LINE = 8
TOKENS = 128
WIDTH = 1024
NARROW = 2048
WIDE = 8192
BOTH = (0, 1)
PAIR = 2
BACK = 3
COLOR_ROWS = 64
SLOTS = 6
ORDER = tuple(zip(map(int, '0102130451023410652317647523647523467567'), map(int, '0010102002311134012240121233232344433444')))


def gelu(z_pre):
    z_val = z_pre.astype(jnp.float32)
    return (z_val * (0.5 * (1.0 + lax.erf(z_val * INV_ROOT_TWO)))).astype(jnp.bfloat16)


def slope_of(z_pre):
    z_val = z_pre.astype(jnp.float32)
    cdf_val = 0.5 * (1.0 + lax.erf(z_val * INV_ROOT_TWO))
    return cdf_val + z_val * jnp.exp(-0.5 * z_val * z_val) * INV_ROOT_TWO_PI


def reduce_kernel(hid_two, hid_one, z_two, z_one, grad_out, x_two, x_one, w2_out, w2_in, w1_out,
                  ring_ref, own_ref, last_ref, dz_out, dx_two, land_w, land_n,
                  stage_w, stage_n, part, got1, got2, got3, got4, dz_buf, dy_buf, dx_buf, z_buf,
                  xs_n, xr_n, xs_w, xr_w, stage_sem_w, stage_sem_n, rs_send, rs_recv, z_sem, put_sem):
    narrows = (grad_out, x_two, dx_two, x_one)

    def wide_piece(m, line, h):
        if m % PAIR:
            return dz_out.at[m // PAIR, PAIR * line + h]
        return (hid_two, hid_one)[m // PAIR].at[:, pl.ds(pl.multiple_of(line * WIDTH + h * HALF, HALF), HALF)]

    def fetch_tile(which, t):
        slot = t % PAIR
        if which == 1:
            def columns(k, carry):
                pltpu.make_async_copy(w2_in.at[pl.ds(PAIR * t, PAIR), :, pl.ds(pl.multiple_of(k * NARROW, NARROW), NARROW)],
                                      stage_n.at[slot, pl.ds(PAIR * k, PAIR)], stage_sem_n.at[slot]).start()
                return carry
            lax.fori_loop(0, 4, columns, 0)
        else:
            pltpu.make_async_copy((w2_out, None, w1_out)[which].at[pl.ds(8 * t, 8)], stage_n.at[slot], stage_sem_n.at[slot]).start()
            z_pre = (z_two, None, z_one)[which]
            pltpu.make_async_copy(z_pre.at[:, pl.ds(pl.multiple_of(t * WIDTH, WIDTH), WIDTH)], z_buf.at[slot], z_sem.at[slot]).start()

    def tiles(which, body):
        def step(t, carry):
            slot = t % PAIR
            pltpu.make_async_copy(stage_n.at[slot], stage_n.at[slot], stage_sem_n.at[slot]).wait()
            if which != 1:
                pltpu.make_async_copy(z_buf.at[slot], z_buf.at[slot], z_sem.at[slot]).wait()
            body(t, slot)

            @pl.when(t < 6)
            def _():
                fetch_tile(which, t + PAIR)
            if which < PAIR:
                @pl.when(t >= 6)
                def _():
                    fetch_tile(which + 1, t - 6)
            return carry
        lax.fori_loop(0, 8, step, 0)

    def weights(slot, pair):
        return stage_n[slot, PAIR * pair:PAIR * pair + PAIR].reshape(256, NARROW)

    def grad_pre(which, grad_ref):
        def body(t, slot):
            for pair in range(4):
                grad_hidden = lax.dot_general(grad_ref[...], weights(slot, pair), CONTRACT_COLS, preferred_element_type=jnp.float32)
                at = 256 * (pair % PAIR)
                slope = slope_of(z_buf[slot, :, 256 * pair:256 * pair + 256])
                dz_buf[PAIR * t + pair // PAIR, :, at:at + 256] = (grad_hidden * slope).astype(jnp.bfloat16)
        tiles(which, body)
        put = pltpu.make_async_copy(dz_buf, dz_out.at[which // PAIR], put_sem.at[0])
        put.start()
        put.wait()

    def grad_input():
        def body(t, slot):
            total = None
            for k in range(16):
                at = HALF * (k % CHIPS)
                prod = lax.dot_general(dz_buf[k], weights(slot, k // 4)[:, at:at + HALF], CONTRACT_COLS, preferred_element_type=jnp.float32)
                total = prod if total is None else total + prod
            cols = pl.ds(pl.multiple_of(t * 256, 256), 256)
            dx_buf[:, cols] = (dy_buf[:, cols].astype(jnp.float32) + total).astype(jnp.bfloat16)
        tiles(1, body)
        put = pltpu.make_async_copy(dx_buf, dx_two, put_sem.at[1])
        put.start()
        put.wait()

    fetch_tile(0, 0)
    fetch_tile(0, 1)
    get_dy = pltpu.make_async_copy(grad_out, dy_buf, put_sem.at[1])
    get_dy.start()
    z, y, g = lax.axis_index('third'), lax.axis_index('second'), lax.axis_index('group')
    x, c = g // PAIR, g % PAIR
    pos = {'x': x, 'y': y, 'z': z}

    def device(axis, off, core):
        at = dict(pos)
        at[axis] = (pos[axis] + off) % CHIPS
        return (at['z'], at['y'], PAIR * at['x'] + core)

    barrier = pltpu.get_barrier_semaphore()
    peers = [device(axis, off, core) for axis in 'xyz' for off in (1, PAIR, BACK) for core in BOTH] + [device('x', 0, 1 - c)]
    for peer in peers:
        pl.semaphore_signal(barrier, inc=1, device_id=peer, device_id_type=MESH)
    pl.semaphore_wait(barrier, len(peers))

    def line_index(m):
        return PAIR * pos[ROLES[m][0]] + c

    def direct_narrow(m, off, core):
        return pltpu.make_async_remote_copy(
            src_ref=narrows[m], dst_ref=land_n.at[m, line_index(m)], send_sem=xs_n.at[m, off], recv_sem=xr_n.at[m, line_index(m)],
            device_id=device(ROLES[m][0], off, core), device_id_type=MESH)

    def relay_narrow(m, off):
        source = PAIR * ((pos[ROLES[m][0]] + off) % CHIPS) + c
        return pltpu.make_async_remote_copy(
            src_ref=land_n.at[m, source], dst_ref=land_n.at[m, source], send_sem=xs_n.at[m, BACK + off], recv_sem=xr_n.at[m, source],
            device_id=device('x', 0, 1 - c), device_id_type=MESH)

    def wide_copy(m, h, off, core):
        me = line_index(m)
        target = PAIR * ((pos[ROLES[m][0]] + off) % CHIPS) + core
        return pltpu.make_async_remote_copy(
            src_ref=wide_piece(m, target, h), dst_ref=land_w.at[m, h, me], send_sem=xs_w.at[m, h, PAIR * off + core], recv_sem=xr_w.at[m, h, me],
            device_id=device(ROLES[m][0], off, core), device_id_type=MESH)

    def over_chips(fn):
        lax.fori_loop(1, 4, lambda off, carry: (fn(off), carry)[1], 0)

    def start_narrow(m):
        over_chips(lambda off: direct_narrow(m, off, c).start())
        direct_narrow(m, 0, 1 - c).start()

    def start_wide(m, h):
        def both(off):
            wide_copy(m, h, off, 0).start()
            wide_copy(m, h, off, 1).start()
        over_chips(both)
        wide_copy(m, h, 0, 1 - c).start()

    def relay(m):
        def one(off):
            source = PAIR * ((pos[ROLES[m][0]] + off) % CHIPS) + c
            pltpu.make_async_copy(land_n.at[m, source], land_n.at[m, source], xr_n.at[m, source]).wait()
            relay_narrow(m, off).start()
        over_chips(one)

    def wait_exchange_sends(m):
        over_chips(lambda off: direct_narrow(m, off, c).wait_send())
        direct_narrow(m, 0, 1 - c).wait_send()
        over_chips(lambda off: relay_narrow(m, off).wait_send())
        for h in BOTH:
            def both(off):
                wide_copy(m, h, off, 0).wait_send()
                wide_copy(m, h, off, 1).wait_send()
            over_chips(both)
            wide_copy(m, h, 0, 1 - c).wait_send()

    def stage_narrow(m):
        me = line_index(m)
        slot = m % PAIR

        def other_core(off, carry):
            source = PAIR * ((pos[ROLES[m][0]] + off) % CHIPS) + 1 - c
            pltpu.make_async_copy(land_n.at[m, source], land_n.at[m, source], xr_n.at[m, source]).wait()
            return carry
        lax.fori_loop(0, 4, other_core, 0)

        def fetch(off, carry):
            source = (me + off) % LINE
            pltpu.make_async_copy(land_n.at[m, source], stage_n.at[slot, source], stage_sem_n.at[slot]).start()
            return carry
        lax.fori_loop(1, LINE, fetch, 0)
        pltpu.make_async_copy(narrows[m], stage_n.at[slot, me], stage_sem_n.at[slot]).start()

    def stage_wide(m, h):
        me = line_index(m)

        def fetch(off, carry):
            source = (me + off) % LINE
            pltpu.make_async_copy(land_w.at[m, h, source], land_w.at[m, h, source], xr_w.at[m, h, source]).wait()
            pltpu.make_async_copy(land_w.at[m, h, source], stage_w.at[h, source], stage_sem_w.at[h]).start()
            return carry
        lax.fori_loop(1, LINE, fetch, 0)
        pltpu.make_async_copy(wide_piece(m, me, h), stage_w.at[h, me], stage_sem_w.at[h]).start()

    def rs_copy(j, color, stage, side):
        m, h = j // PAIR, j % PAIR
        first, second = ROLES[m][1:] if color == 0 else ROLES[m][:0:-1]
        p, q = pos[first], pos[second]
        slot, got = j % SLOTS, j % 6
        sign = 1 if side == 0 else BACK
        mine = part.at[slot, color]
        if stage == 1:
            src, dst, axis = mine.at[(p + PAIR) % CHIPS, pl.ds(PAIR * side, PAIR)], got1.at[got, color, side], first
        elif stage == PAIR:
            src, dst, axis = mine.at[(p + sign) % CHIPS], got2.at[got, color, side], first
        elif stage == BACK:
            src, dst, axis = mine.at[p, (q + PAIR) % CHIPS, pl.ds(32 * side, 32)], got3.at[got, color, side], second
        else:
            src, dst, axis = mine.at[p, (q + sign) % CHIPS], got4.at[got, color, side], second
        return pltpu.make_async_remote_copy(
            src_ref=src, dst_ref=dst, send_sem=rs_send.at[j, color, stage - 1, side], recv_sem=rs_recv.at[j, color, stage - 1, side],
            device_id=device(axis, sign, c), device_id_type=MESH)

    def compute(j):
        m, h = j // PAIR, j % PAIR
        slot = j % SLOTS
        a, b = pos[ROLES[m][1]], pos[ROLES[m][PAIR]]
        if h == 0:
            pltpu.make_async_copy(stage_n.at[m % PAIR], stage_n.at[m % PAIR], stage_sem_n.at[m % PAIR]).wait()
        pltpu.make_async_copy(stage_w.at[h], stage_w.at[h], stage_sem_w.at[h]).wait()
        wide, narrow = stage_w.at[h], stage_n.at[m % PAIR]

        def piece(i, carry):
            k = jnp.maximum(i - 7, 0)
            pa = jnp.where(i < 4, a + PAIR, jnp.where(i < 7, a + i - 1, a + BACK + k // BACK)) % CHIPS
            pb = jnp.where(i < 4, i, jnp.where(i < 7, b + PAIR, b + BACK + k % BACK)) % CHIPS
            if m % PAIR == 0:
                lhs, lhs_at, rhs, rhs_at = wide, pa * TOKENS, narrow, pb * HALF
            else:
                lhs, lhs_at, rhs, rhs_at = narrow, (pa * 4 + pb) * TOKENS, wide, 0
            lhs_cols = pl.ds(pl.multiple_of(lhs_at, TOKENS), TOKENS)
            rhs_cols = pl.ds(pl.multiple_of(rhs_at, HALF), HALF) if m % PAIR == 0 else slice(None)
            total = None
            for dev in range(8):
                prod = lax.dot_general(lhs[dev, :, lhs_cols], rhs[dev, :, rhs_cols], CONTRACT_ROWS, preferred_element_type=jnp.float32)
                prod = prod.astype(jnp.bfloat16).astype(jnp.float32)
                total = prod if total is None else total + prod
            part[slot, 0, pa, pb] = total[:COLOR_ROWS]
            part[slot, 1, pb, pa] = total[COLOR_ROWS:]

            @pl.when(i == BACK)
            def _():
                rs_copy(j, 0, 1, 0).start()
                rs_copy(j, 0, 1, 1).start()

            @pl.when(i == 6)
            def _():
                rs_copy(j, 1, 1, 0).start()
                rs_copy(j, 1, 1, 1).start()
            return carry
        lax.fori_loop(0, 16, piece, 0)

    def coords(j, color):
        m = j // PAIR
        first, second = ROLES[m][1:] if color == 0 else ROLES[m][:0:-1]
        return pos[first], pos[second]

    def stage_two(j):
        slot, got = j % SLOTS, j % 6
        for color in BOTH:
            p, q = coords(j, color)
            rs_copy(j, color, 1, 0).wait_recv()
            part[slot, color, (p + 1) % CHIPS, 0:PAIR] += got1[got, color, 0]
            rs_copy(j, color, 1, 1).wait_recv()
            part[slot, color, (p + BACK) % CHIPS, PAIR:4] += got1[got, color, 1]
            rs_copy(j, color, PAIR, 0).start()
            rs_copy(j, color, PAIR, 1).start()

    def stage_three(j):
        slot, got = j % SLOTS, j % 6
        for color in BOTH:
            p, q = coords(j, color)
            rs_copy(j, color, PAIR, 0).wait_recv()
            rs_copy(j, color, PAIR, 1).wait_recv()
            part[slot, color, p] += got2[got, color, 0] + got2[got, color, 1]
        for color in BOTH:
            rs_copy(j, color, BACK, 0).start()
            rs_copy(j, color, BACK, 1).start()

    def stage_four(j):
        slot, got = j % SLOTS, j % 6
        for color in BOTH:
            p, q = coords(j, color)
            rs_copy(j, color, BACK, 0).wait_recv()
            part[slot, color, p, (q + 1) % CHIPS, 0:32] += got3[got, color, 0]
            rs_copy(j, color, BACK, 1).wait_recv()
            part[slot, color, p, (q + BACK) % CHIPS, 32:COLOR_ROWS] += got3[got, color, 1]
            rs_copy(j, color, 4, 0).start()
            rs_copy(j, color, 4, 1).start()

    def stage_five(j):
        m, h = j // PAIR, j % PAIR
        slot, got = j % SLOTS, j % 6
        for color in BOTH:
            p, q = coords(j, color)
            rs_copy(j, color, 4, 0).wait_recv()
            rs_copy(j, color, 4, 1).wait_recv()
            if m < PAIR:
                out_ref = ring_ref.at[m, pl.ds(COLOR_ROWS * color, COLOR_ROWS)]
            elif m == BACK:
                out_ref = own_ref.at[color]
            else:
                out_ref = last_ref.at[0] if color else own_ref.at[PAIR]
            out_ref[:, h * HALF:(h + 1) * HALF] = part[slot, color, p, q] + got4[got, color, 0] + got4[got, color, 1]

    def drain(j):
        for color in BOTH:
            for stage in (1, PAIR, BACK, 4):
                for side in BOTH:
                    rs_copy(j, color, stage, side).wait_send()

    start_narrow(0)
    start_narrow(1)
    for h in BOTH:
        start_wide(0, h)
    for h in BOTH:
        start_wide(PAIR, h)
    start_narrow(BACK)
    get_dy.wait()
    grad_pre(0, dy_buf)
    for h in BOTH:
        start_wide(1, h)
    grad_input()
    start_narrow(PAIR)
    relay(0)
    relay(1)
    grad_pre(PAIR, dx_buf)
    for h in BOTH:
        start_wide(BACK, h)
    stage_narrow(0)
    stage_wide(0, 0)

    def compute_step(j):
        if j == 6:
            relay(BACK)
            stage_narrow(BACK)
            stage_wide(BACK, 0)
        if j >= SLOTS:
            drain(j - SLOTS)
        if j + 1 < 8 and j + 1 != 6:
            if j + 1 == 4:
                relay(PAIR)
            if (j + 1) % PAIR == 0:
                stage_narrow((j + 1) // PAIR)
            stage_wide((j + 1) // PAIR, (j + 1) % PAIR)
        compute(j)

    steps = (compute_step, stage_two, stage_three, stage_four, stage_five)
    for job, stage in ORDER:
        steps[stage](job)
    for j in range(8 - SLOTS, 8):
        drain(j)
    for m in range(4):
        wait_exchange_sends(m)


def reduce_factors(*operands):
    f32, bf16, dma = jnp.float32, jnp.bfloat16, pltpu.SemaphoreType.DMA
    any_spec = pl.BlockSpec(memory_space=pl.ANY)
    vmem_spec = pl.BlockSpec(memory_space=pltpu.VMEM)
    return pl.pallas_call(
        reduce_kernel,
        out_shape=(jax.ShapeDtypeStruct((PAIR, TOKENS, WIDTH), f32), jax.ShapeDtypeStruct((BACK, COLOR_ROWS, WIDTH), f32), jax.ShapeDtypeStruct((1, COLOR_ROWS, WIDTH), f32),
                   jax.ShapeDtypeStruct((PAIR, 16, TOKENS, HALF), bf16), jax.ShapeDtypeStruct((TOKENS, NARROW), bf16),
                   jax.ShapeDtypeStruct((4, PAIR, 8, TOKENS, HALF), bf16), jax.ShapeDtypeStruct((4, 8, TOKENS, NARROW), bf16)),
        in_specs=[any_spec] * len(operands),
        out_specs=(vmem_spec,) * BACK + (any_spec,) * 4,
        scratch_shapes=[
            pltpu.VMEM((PAIR, 8, TOKENS, HALF), bf16), pltpu.VMEM((PAIR, 8, TOKENS, NARROW), bf16),
            pltpu.VMEM((SLOTS, PAIR, 4, 4, COLOR_ROWS, HALF), f32),
            pltpu.VMEM((6, PAIR, PAIR, PAIR, COLOR_ROWS, HALF), f32), pltpu.VMEM((6, PAIR, PAIR, 4, COLOR_ROWS, HALF), f32),
            pltpu.VMEM((6, PAIR, PAIR, 32, HALF), f32), pltpu.VMEM((6, PAIR, PAIR, COLOR_ROWS, HALF), f32),
            pltpu.VMEM((16, TOKENS, HALF), bf16), pltpu.VMEM((TOKENS, NARROW), bf16), pltpu.VMEM((TOKENS, NARROW), bf16), pltpu.VMEM((PAIR, TOKENS, WIDTH), bf16),
            dma((4, 8)), dma((4, 8)), dma((4, PAIR, 8)), dma((4, PAIR, 8)), dma((PAIR,)), dma((PAIR,)),
            dma((8, PAIR, 4, PAIR)), dma((8, PAIR, 4, PAIR)), dma((PAIR,)), dma((PAIR,)),
        ],
        compiler_params=pltpu.CompilerParams(collective_id=0, has_side_effects=True, vmem_limit_bytes=67043328),
        cost_estimate=pl.CostEstimate(flops=1 << 34, bytes_accessed=COLOR_ROWS << 20, transcendentals=0),
        name='reduce_factors',
    )(*operands)[:5]


def gather_kernel(own_ref, whole0, whole1, whole2, held, get_sem, put_sem, send_sem, recv_sem):
    wholes = (whole0, whole1, whole2)
    z, y, g = lax.axis_index('third'), lax.axis_index('second'), lax.axis_index('group')
    x, c = g // PAIR, g % PAIR
    pos = {'x': x, 'y': y, 'z': z}

    def device(axis, off, core):
        at = dict(pos)
        at[axis] = (pos[axis] + off) % CHIPS
        return (at['z'], at['y'], PAIR * at['x'] + core)

    gets = [pltpu.make_async_copy(own_ref.at[i], held.at[i], get_sem.at[i]) for i in range(BACK)]
    for get in gets:
        get.start()
    barrier = pltpu.get_barrier_semaphore()
    peers = [device(axis, off, c) for axis in 'xyz' for off in (1, BACK)] + [device('x', 0, 1 - c)]
    for peer in peers:
        pl.semaphore_signal(barrier, inc=1, device_id=peer, device_id_type=MESH)
    pl.semaphore_wait(barrier, len(peers))

    def copy(i, n):
        axes = GATHER[i]
        p1, p2, p3 = [pos[axis] for axis in axes]
        mine = wholes[i].at[c]
        side = n % PAIR
        back = BACK - PAIR * side
        rows = (p2, (p2 + BACK) % CHIPS, (p2 + 1) % CHIPS, (p2 + PAIR) % CHIPS)
        src = None
        axis, off = axes[0], 1 + PAIR * side
        if n < PAIR:
            dst, src = mine.at[p3, p2, p1], held.at[i]
        elif n < 4:
            dst = mine.at[p3, p2, (p1 + back) % CHIPS, pl.ds(32 * side, 32)]
        elif n < 6:
            axis, dst = axes[1], mine.at[p3, p2]
        elif n < 8:
            axis, dst = axes[1], mine.at[p3, (p2 + back) % CHIPS, pl.ds(PAIR * side, PAIR)]
        elif n < 16:
            axis, dst = axes[PAIR], mine.at[p3, rows[(n - 8) // PAIR]]
        elif n < 20:
            axis, dst = axes[PAIR], mine.at[(p3 + back) % CHIPS, rows[PAIR * side + (n - 16) // PAIR]]
        else:
            axis, off, dst = axes[PAIR], 0, mine.at[(p3, (p3 + BACK) % CHIPS, (p3 + 1) % CHIPS, (p3 + PAIR) % CHIPS)[(n - 20) // 4], rows[n % CHIPS]]
        return pltpu.make_async_remote_copy(
            src_ref=dst if src is None else src, dst_ref=dst, send_sem=send_sem.at[i, n], recv_sem=recv_sem.at[i, n],
            device_id=device(axis, off, c if n < 20 else 1 - c), device_id_type=MESH)

    def start(i, *which):
        for n in which:
            copy(i, n).start()

    def wait(i, *which):
        for n in which:
            copy(i, n).wait_recv()

    puts = []
    for i in range(BACK):
        p1, p2, p3 = [pos[axis] for axis in GATHER[i]]
        gets[i].wait()
        start(i, 0, 1)
        puts.append(pltpu.make_async_copy(held.at[i], wholes[i].at[c, p3, p2, p1], put_sem.at[i]))
        puts[i].start()
    for i in range(BACK):
        for side in BOTH:
            wait(i, side)
            start(i, PAIR + side)
    for i in range(BACK):
        puts[i].wait()
        wait(i, PAIR, BACK)
        start(i, 4, 5, 20)
    for i in range(BACK):
        for side in BOTH:
            wait(i, 4 + side)
            start(i, 6 + side)
    for k in range(BACK):
        for i in range(BACK):
            start(i, 8 + PAIR * k, 9 + PAIR * k)
            if k:
                start(i, 20 + k)
    for i in range(BACK):
        wait(i, 6, 7)
        start(i, 14, 15, 23)
    for k in range(4):
        for i in range(BACK):
            for side in BOTH:
                wait(i, 8 + PAIR * k + side)
                if k // PAIR == side:
                    start(i, 16 + PAIR * (k % PAIR) + side)
                start(i, 24 + 4 * side + k)
    for k in range(PAIR):
        for i in range(BACK):
            for side in BOTH:
                wait(i, 16 + PAIR * k + side)
                start(i, 32 + PAIR * side + k)
    for i in range(BACK):
        wait(i, *range(20, 36))
        for n in range(36):
            copy(i, n).wait_send()


def gather_own(own):
    f32, dma = jnp.float32, pltpu.SemaphoreType.DMA
    any_spec = pl.BlockSpec(memory_space=pl.ANY)
    return pl.pallas_call(
        gather_kernel,
        out_shape=(jax.ShapeDtypeStruct((PAIR, 4, 4, 4, COLOR_ROWS, WIDTH), f32),) * BACK,
        in_specs=[any_spec],
        out_specs=(any_spec,) * BACK,
        scratch_shapes=[pltpu.VMEM((BACK, COLOR_ROWS, WIDTH), f32), dma((BACK,)), dma((BACK,)), dma((BACK, 36)), dma((BACK, 36))],
        compiler_params=pltpu.CompilerParams(collective_id=1, has_side_effects=True),
        cost_estimate=pl.CostEstimate(flops=1 << 38, bytes_accessed=96 << 20, transcendentals=0),
        name='gather_own',
    )(own)


def columns_kernel(pick, in_ref, *rest):
    out_ref = rest[-1]
    for q in range(4):
        for line in range(out_ref.shape[0]):
            for h in BOTH:
                out_ref[line, h, 0, :, q * HALF:(q + 1) * HALF] = in_ref[pick(q, line)][:, h * HALF:(h + 1) * HALF]


def rows_kernel(picks, *refs):
    out_ref = refs[-1]
    for e in range(4):
        for core in BOTH:
            at = (PAIR * e + core) * WIDTH
            for pick, in_ref in zip(picks, refs):
                piece = in_ref[pick(e, core)]
                first = len(piece) * picks.index(pick)
                out_ref[first:first + len(piece), at:at + WIDTH] = piece


def place(kernel, grid, blocks, arrays, out_shape, out_block, out_index, into=None):
    in_specs = [pl.BlockSpec(block, index) for block, index in blocks]
    if into is not None:
        in_specs.append(pl.BlockSpec(memory_space=pl.ANY))
        arrays = arrays + (into,)
    return pl.pallas_call(
        kernel, grid=grid, in_specs=in_specs, out_specs=pl.BlockSpec(out_block, out_index),
        out_shape=jax.ShapeDtypeStruct(out_shape, jnp.float32),
        input_output_aliases={} if into is None else {len(in_specs) - 1: 0},
        cost_estimate=pl.CostEstimate(flops=1 << 30, bytes_accessed=TOKENS << 20, transcendentals=0), name='place',
    )(*arrays)


OUT_SHAPE = (8, PAIR, 4, TOKENS, NARROW)


def place_zero(ring):
    return place(functools.partial(columns_kernel, lambda q, line: (q, 0, 0, line, 0)), (4, 4),
                 [((4, 1, 1, PAIR, 1, TOKENS, WIDTH), lambda i, k: (0, i, k, 0, 0, 0, 0))], (ring,),
                 OUT_SHAPE, (PAIR, PAIR, 1, TOKENS, NARROW), lambda i, k: (k, 0, i, 0, 0)).reshape(WIDE, NARROW)


def place_one(ring):
    return place(functools.partial(rows_kernel, (lambda e, core: (0, e, 0, core, 0),)), (4, 4),
                 [((1, 4, 1, PAIR, 1, TOKENS, WIDTH), lambda i, k: (i, 0, k, 0, 1, 0, 0))], (ring,),
                 (NARROW, WIDE), (TOKENS, WIDE), lambda i, k: (4 * i + k, 0))


def place_two_low(piece):
    return place(functools.partial(columns_kernel, lambda q, line: (line % PAIR, line // PAIR, q, 0)), (4, PAIR),
                 [((PAIR, PAIR, 4, 1, COLOR_ROWS, WIDTH), lambda i, k: (0, k, 0, i, 0, 0))], (piece,),
                 OUT_SHAPE, (4, PAIR, 1, COLOR_ROWS, NARROW), lambda i, k: (k, 0, i, 0, 0))


def place_two_high(ring, low):
    return place(functools.partial(columns_kernel, lambda q, line: (line // PAIR, q, 0, line % PAIR, 0)), (4, PAIR),
                 [((PAIR, 4, 1, PAIR, 1, COLOR_ROWS, WIDTH), lambda i, k: (k, 0, i, 0, 0, 0, 0))], (ring,),
                 OUT_SHAPE, (4, PAIR, 1, COLOR_ROWS, NARROW), lambda i, k: (k, 0, i, 1, 0), low).reshape(WIDE, NARROW)


def place_three(low, high):
    return place(functools.partial(rows_kernel, (lambda e, core: (core, e, 0, 0), lambda e, core: (core, 0, e, 0))), (4, 4),
                 [((PAIR, 4, 1, 1, COLOR_ROWS, WIDTH), lambda i, k: (0, 0, k, i, 0, 0)), ((PAIR, 1, 4, 1, COLOR_ROWS, WIDTH), lambda i, k: (0, i, 0, k, 0, 0))],
                 (low, high), (NARROW, WIDE), (TOKENS, WIDE), lambda i, k: (4 * i + k, 0))


def solution(mesh):
    def device_step(x_one, z_one, x_two, z_two, grad_out, w1_in, w1_out, w2_in, w2_out):
        ring, own, last, grad_pre, dx_two = reduce_factors(
            gelu(z_two), gelu(z_one), z_two, z_one, grad_out, x_two, x_one,
            w2_out.reshape(COLOR_ROWS, TOKENS, NARROW), w2_in.reshape(16, TOKENS, WIDE), w1_out.reshape(COLOR_ROWS, TOKENS, NARROW))
        dz_one = grad_pre[1].transpose(1, 0, PAIR).reshape(TOKENS, WIDE)
        dx_one = (dx_two.astype(jnp.float32) + lax.dot_general(dz_one, w1_in, CONTRACT_COLS, preferred_element_type=jnp.float32)).astype(jnp.bfloat16)

        def gather(part):
            whole = lax.all_gather(part, AXES, axis=0)
            return whole.reshape(CHIPS, CHIPS, CHIPS, PAIR, *part.shape)

        first = gather(ring)
        three_low, three_high, two_low = gather_own(own)
        sum_three = place_three(three_low, three_high)
        sum_two = place_two_low(two_low)
        last, first, sum_two, sum_three = lax.optimization_barrier((last, first, sum_two, sum_three))
        sum_two = place_two_high(gather(last), sum_two)
        return (place_zero(first), place_one(first), sum_two, sum_three, dx_one)

    row_spec = P(AXES, None)
    repl_spec = P()
    return jax.shard_map(
        device_step, mesh=mesh,
        in_specs=(row_spec,) * 5 + (repl_spec,) * 4,
        out_specs=(repl_spec,) * 4 + (row_spec,),
        check_vma=False,
    )
```

time: 833 us -> 783 us (0.940)
  waiting for transfers between devices: 410 us -> 11.3 us
  Pallas kernels: 379 us -> 727 us
    all_gather x2, waiting for transfers between devices: 410 us -> 11.3 us  [gather(): whole = lax.all_gather(part, AXES, axis=0)]
    pallas_call x5 -> x7, Pallas kernels: 379 us -> 727 us  [the longest x1 348 us: gather_own(): pl.pallas_call(gather_kernel, out_shape=(jax.ShapeDtypeStruct((PAIR, 4, 4...]
  transfers between devices with their start and end apart: 2 -> 2, of which waited for: 2 -> 1; matrix products, arithmetic and copies ran while one was open for 3% -> 3% of each run, Pallas kernels for 16% -> 65%
where the time goes in v3:
time: 783 us; the launch traced here: 782 us
  Pallas kernels  727 us (93%)
  matrix products  17 us (2%)
  between operations  14.1 us (2%)
  waiting for transfers between devices  11.3 us (1%)
    pallas_call x1, Pallas kernels, gather_own(): pl.pallas_call(gather_kernel, out_shape=(jax.ShapeDtypeStruct((PAIR, 4, 4...  348 us
    pallas_call x1, Pallas kernels, reduce_factors(): pl.pallas_call(reduce_kernel, out_shape=(jax.ShapeDtypeStruct((PAIR, TOKE...  200 us
    pallas_call x5, Pallas kernels, place(): pl.pallas_call(kernel, grid=grid, in_specs=in_specs, out_specs=pl.BlockSp...  180 us
    dot_general x1, matrix products, device_step(): lax.dot_general(dz_one, w1_in, CONTRACT_COLS, preferred_element_type=jnp....  17 us
  transfers between devices with their start and end apart: 2, of which 1 were waited for; matrix products, arithmetic and copies ran while one was open for 3% of the time, Pallas kernels for 65%

profile of v3, /device:TPU:1, one launch (start us, length us, event | category | flops | bytes accessed | tf_op | source)
XLA Modules:
  0.0 781.6 jit_solution(1818126025775630642)
XLA Ops:
  7.2 0.0 all-gather.5.cloned.1.call-start
  7.2 5.5 fusion.3
  12.7 199.8 %reduce_factors.1 = (f32[2,128,1024]{2,1,0:T(8,128)}, f32[3,64,1024]{2,1,0:T(8,128)}, f32[1,64,1024]{2,1,0:T(8,128)}, bf16[2,16,128,512]{3,2,1,0:T(8,128)(2,1)},...) custom-call(bf16[128,8192]{1,0:T(8,128)(2,1)} %get-tuple-element.29.hid_two, ...), custom_call_target="tpu_custom_call" | custom-call | flops 17179869184 | bytes 67108864 | tf_op jit(solution)/shard_map/reduce_factors/pallas_call | solution.py:381
  212.5 0.0 all-gather.5.cloned.1.call-update
  212.5 0.2 all-gather.7.cloned.1.call-start
  212.8 347.8 %gather_own.1 = (f32[2,4,4,4,64,1024]{5,4,3,2,1,0:T(8,128)}, f32[2,4,4,4,64,1024]{5,4,3,2,1,0:T(8,128)}, f32[2,4,4,4,64,1024]{5,4,3,2,1,0:T(8,128)}) custom-call(f32[3,64,1024]{2,1,0:T(8,128)} %get-tuple-element.19.own_ref), custom_call_target="tpu_custom_call" | custom-call | flops 274877906944 | bytes 100663296 | tf_op jit(solution)/shard_map/gather_own/pallas_call | solution.py:506
  560.6 22.6 %place.5.rest_0_ = f32[8,2,4,128,2048]{4,3,2,1,0:T(8,128)} custom-call(f32[2,4,4,4,64,1024]{5,4,3,2,1,0:T(8,128)} %get-tuple-element.20.in_ref), custom_call_target="tpu_custom_call" | custom-call | flops 1073741824 | bytes 134217728 | tf_op jit(solution)/shard_map/place/pallas_call | solution.py:542
  583.2 45.1 %place.6 = f32[2048,8192]{1,0:T(8,128)} custom-call(f32[2,4,4,4,64,1024]{5,4,3,2,1,0:T(8,128)} %get-tuple-element.21.refs_0_, f32[2,4,4,4,64,1024]{5,4,3,2,1,0:T(8,128)} %get-tuple-element.22.refs_1_), custom_call_target="tpu_custom_call" | custom-call | flops 1073741824 | bytes 134217728 | tf_op jit(solution)/shard_map/place/pallas_call | solution.py:542
  628.3 11.3 %all-gather.5.cloned.1.call-done = f32[256,128,1024]{2,1,0:T(8,128)} async-done(((f32[2,128,1024]{2,1,0:T(8,128)}), f32[256,128,1024]{2,1,0:T(8,128)}) %all-gather.5.cloned.1.call-update) | async-done | bytes 134217744 | tf_op jit(solution)/shard_map/all_gather | solution.py:592
  639.6 0.0 all-gather.7.cloned.1.call-update
  639.6 0.0 copy-start
  639.6 3.2 slice_bitcast_fusion
  642.8 3.0 copy.16
  645.8 0.0 copy-done
  645.8 17.0 %fusion.8 = bf16[128,2048]{1,0:T(8,128)(2,1)} fusion(bf16[128,8192]{0,1:T(8,128)(2,1)S(1)} %bitcast.18, bf16[2048,8192]{1,0:T(8,128)(2,1)} %param.14, bf16[128,2048]{1,0:T(8,128)(2,1)S(1)} %copy-done), kind=kOutput, calls=%fused_computation.13 | convolution fusion | flops 4295753728 | bytes 36700160 | tf_op jit(solution)/shard_map/dot_general | solution.py:589
  662.8 44.7 %place.8 = f32[2048,8192]{1,0:T(8,128)} custom-call(f32[4,4,4,2,2,128,1024]{6,5,4,3,2,1,0:T(8,128)} %bitcast.3.in_ref.refs_0_), custom_call_target="tpu_custom_call" | custom-call | flops 1073741824 | bytes 134217728 | tf_op jit(solution)/shard_map/place/pallas_call | solution.py:542
  707.5 44.7 %place.7 = f32[8,2,4,128,2048]{4,3,2,1,0:T(8,128)} custom-call(f32[4,4,4,2,2,128,1024]{6,5,4,3,2,1,0:T(8,128)} %bitcast.3.in_ref.refs_0_), custom_call_target="tpu_custom_call" | custom-call | flops 1073741824 | bytes 134217728 | tf_op jit(solution)/shard_map/place/pallas_call | solution.py:542
  752.3 0.0 all-gather.7.cloned.1.call-done
  752.3 22.5 %place.9 = f32[8,2,4,128,2048]{4,3,2,1,0:T(8,128)} custom-call(f32[4,4,4,2,1,64,1024]{6,5,4,3,2,1,0:T(8,128)} %bitcast.14, f32[8,2,4,128,2048]{4,3,2,1,0:T(8,128)} %place.5.rest_0_), custom_call_target="tpu_custom_call", output_to_operand_aliasing={{}: (1, {})} | custom-call | flops 1073741824 | bytes 134217728 | tf_op jit(solution)/shard_map/place/pallas_call | solution.py:542
Async XLA Ops:
  7.2 632.4 %all-gather.5.cloned.1.call-start = ((), (), s32[]{:S(2)}) async-start(), calls=%async_computation | async-start | bytes 135266304 | tf_op jit(solution)/shard_map/all_gather | solution.py:592
  212.5 539.7 %all-gather.7.cloned.1.call-start = ((), (), s32[]{:S(2)}) async-start(), calls=%async_computation.1 | async-start | bytes 33816576 | tf_op jit(solution)/shard_map/all_gather | solution.py:592
  639.6 6.2 copy-start
Sparse Core Ops, SparseCore 0:
  212.6 426.8 all-gather.4
  642.6 104.3 all-gather.6
